TPU v7x, 8 devices: a whole 2x2x1 slice. The times are simulated.
8 devices in a mesh: model: 4 (over z, y, x), data: 2 (over core).
Axes of the slice: x: 2, y: 2, z: 1, core: 2. Of those that a mesh axis runs over, the one named last changes fastest.
Arguments:
- local_grads: bfloat16 [2, 192, 262144], P('data', None, 'model')
- master: float32 [192, 262144], P(None, ('model', 'data'))
- moment_one: float32 [192, 262144], P(None, ('model', 'data'))
- moment_two: float32 [192, 262144], P(None, ('model', 'data'))
Outputs:
- output 1: bfloat16 [192, 262144], P(None, 'model')
- output 2: float32 [192, 262144], P(None, ('model', 'data'))
- output 3: float32 [192, 262144], P(None, ('model', 'data'))
- output 4: float32 [192, 262144], P(None, ('model', 'data'))
All inputs are finite; a program needn't handle non-finite values.
Results may differ from a plain program's by a relative error of at most 0.001.
Values are sent between devices in bfloat16 or wider.
A program may use at most 1 GiB of HBM per device.

v0:
```python
import jax
import jax.numpy as jnp
from jax import lax
from jax.sharding import PartitionSpec as P

STEP = 4
LEARN_RATE = 0.08
BETA_ONE = 0.9
BETA_TWO = 0.999
EPSILON = 1e-6
WEIGHT_DECAY = 0.01
MAX_NORM = 1.0
CORR_ONE = 1.0 - BETA_ONE ** STEP
CORR_TWO = 1.0 - BETA_TWO ** STEP


def tensor_sums(block_values):
    return jnp.stack([block_values[..., 0:3].sum(axis=-1), block_values[..., 3], block_values[..., 4:8].sum(axis=-1), block_values[..., 8:12].sum(axis=-1)], axis=-1)


def spread_tensors(tensor_values):
    lead_shape = tensor_values.shape[:-1]
    pieces = [jnp.broadcast_to(tensor_values[..., tensor_pos:tensor_pos + 1], lead_shape + (block_count,)) for tensor_pos, block_count in enumerate((3, 1, 4, 4))]
    return jnp.concatenate(pieces, axis=-1)


def adam_direction(grad_mean, clip_scale, master, moment_one, moment_two):
    scaled = clip_scale * grad_mean
    new_one = BETA_ONE * moment_one + (1.0 - BETA_ONE) * scaled
    new_two = BETA_TWO * moment_two + (1.0 - BETA_TWO) * scaled * scaled
    direction = (new_one / CORR_ONE) / (jnp.sqrt(new_two / CORR_TWO) + EPSILON) + WEIGHT_DECAY * master
    return new_one, new_two, direction


def block_ratio(norm_sq):
    tensor_norms = jnp.sqrt(tensor_sums(norm_sq.reshape(2, -1, 12)))
    return spread_tensors(tensor_norms[0] / tensor_norms[1]).reshape(-1, 1)


def solution(mesh):
    data_size = mesh.shape['data']
    both_axes = ('model', 'data')
    state_spec = P(None, both_axes)

    def device_step(local_grads, master, moment_one, moment_two):
        grad_slab = local_grads[0]
        received = lax.all_to_all(grad_slab, 'data', 1, 0, tiled=True)
        grad_mean = jnp.sum(received.reshape(data_size, grad_slab.shape[0], -1), axis=0, dtype=jnp.float32) / data_size
        total_sq = lax.psum(jnp.sum(grad_mean * grad_mean), both_axes)
        clip_scale = jnp.minimum(1.0, MAX_NORM / jnp.sqrt(total_sq))
        new_one, new_two, direction = adam_direction(grad_mean, clip_scale, master, moment_one, moment_two)
        norm_sq = lax.psum(jnp.stack([jnp.sum(master * master, axis=1), jnp.sum(direction * direction, axis=1)]), both_axes)
        new_master = master - LEARN_RATE * block_ratio(norm_sq) * direction
        params = lax.all_gather(new_master.astype(jnp.bfloat16), 'data', axis=1, tiled=True)
        return params, new_master, new_one, new_two

    return jax.shard_map(device_step, mesh=mesh, in_specs=(P('data', None, 'model'), state_spec, state_spec, state_spec), out_specs=(P(None, 'model'), state_spec, state_spec, state_spec), check_vma=False)
```

profile of v0, /device:TPU:0, one launch (start us, length us, event | category | flops | bytes accessed | tf_op | source)
XLA Modules:
  0.0 330.0 jit_solution(15398208783143613680)
XLA Ops:
  7.2 0.0 all-gather.2.cloned.1.call-start
  7.2 32.3 %all_to_all.10 = bf16[192,2,32768]{2,1,0:T(2,128)(2,1)} reshape(bf16[1,192,65536]{2,1,0:T(8,128)(2,1)} %param.4) | data formatting | bytes 50331648 | tf_op jit(solution)/shard_map/all_to_all | solution.py:47
  39.5 21.3 %copy.19 = bf16[192,2,32768]{2,0,1:T(8,128)(2,1)S(1)} copy(bf16[192,2,32768]{2,1,0:T(2,128)(2,1)} %all_to_all.10) | data formatting | bytes 50331648 | tf_op jit(solution)/shard_map/all_to_all | solution.py:47
  60.7 26.7 %all_to_all.13 = bf16[192,2,32768]{2,0,1:T(8,128)(2,1)} all-to-all(bf16[192,2,32768]{2,0,1:T(8,128)(2,1)S(1)} %copy.19), channel_id=1, replica_groups=mesh['model'=4,'data'=2] {'data'}, dimensions={1} | all-to-all | bytes 50331648 | tf_op jit(solution)/shard_map/all_to_all | solution.py:47
  87.4 23.9 %convert_reduce_fusion = f32[192,32768]{1,0:T(8,128)} fusion(bf16[192,2,32768]{2,0,1:T(8,128)(2,1)} %all_to_all.13), kind=kLoop, calls=%fused_computation | loop fusion | flops 18874368 | bytes 50331648 | tf_op jit(solution)/shard_map/reduce_sum | solution.py:48
  111.3 12.1 %multiply_reduce_fusion.1 = f32[]{:T(128)} fusion(f32[192,32768]{1,0:T(8,128)} %convert_reduce_fusion), kind=kLoop, calls=%fused_computation.7 | loop fusion | flops 18874368 | bytes 25165828 | tf_op jit(solution)/shard_map/reduce_sum | solution.py:49
  123.5 25.0 %psum.14 = f32[]{:T(128)} all-reduce(f32[]{:T(128)} %multiply_reduce_fusion.1), channel_id=1, replica_groups=mesh['model'=4,'data'=2] {'model','data'}, use_global_device_ids=true, to_apply=%region_3.0 | all-reduce | flops 1 | bytes 8 | tf_op jit(solution)/shard_map/psum | solution.py:49
  149.2 52.4 %multiply_reduce_fusion.2 = (f32[192]{0:T(256)S(1)}, f32[192]{0:T(256)S(1)}, f32[192,32768]{1,0:T(8,128)}, f32[192,32768]{1,0:T(8,128)}) fusion(f32[192,32768]{1,0:T(8,128)} %param.5, f32[192,32768]{1,0:T(8,128)} %convert_reduce_fusion, f32[]{:T(128)S(6)} %mul.76, f32[192,32768]{1,0:T(8,128)} %param.6, f32[192,32768]{1,0:T(8,128)} %param.7), kind=kLoop, calls=%fused_computation.8 | loop fusion | flops 113245824 | bytes 150996480 | tf_op jit(solution)/shard_map/reduce_sum | solution.py:52
  201.5 0.1 reshape.28
  201.6 23.5 %psum.15 = f32[2,16,12]{2,1,0:T(8,128)S(1)} all-reduce(f32[2,16,12]{2,1,0:T(8,128)S(1)} %reshape.28), channel_id=1, replica_groups=mesh['model'=4,'data'=2] {'model','data'}, use_global_device_ids=true, to_apply=%region_5.0 | all-reduce | flops 384 | bytes 3072 | tf_op jit(solution)/shard_map/psum | solution.py:52
  225.1 0.1 slice_reduce_fusion.2
  225.2 0.2 slice_reduce_fusion.1
  225.4 0.1 slice.41
  225.4 0.1 copy.21
  225.6 0.1 copy.24
  225.7 0.1 broadcast_in_dim.22
  225.7 0.1 broadcast_in_dim.26
  225.8 0.1 broadcast_in_dim.24
  225.9 0.1 maximum_multiply_fusion
  226.0 0.1 mul.91
  226.1 37.1 %fusion.2 = (bf16[192,32768]{1,0:T(8,128)(2,1)}, f32[192,32768]{1,0:T(8,128)}) fusion(f32[192,32768]{1,0:T(8,128)} %param.5, f32[192,32768]{1,0:T(8,128)} %get-tuple-element.23, f32[192,32768]{1,0:T(8,128)} %get-tuple-element.22, f32[192]{0:T(256)S(1)} %mul.91), kind=kLoop, calls=%fused_computation.20 | loop fusion | flops 56623104 | bytes 113246976 | tf_op jit(solution)/shard_map/convert_element_type | solution.py:54
  263.1 0.0 all-gather.2.cloned.1.call-update
  263.1 39.5 %all-gather.2.cloned.1.call-done = bf16[192,65536]{1,0:T(8,128)(2,1)} async-done(((bf16[192,32768]{1,0:T(8,128)(2,1)}), bf16[192,65536]{1,0:T(8,128)(2,1)}) %all-gather.2.cloned.1.call-update) | async-done | bytes 25165840 | tf_op jit(solution)/shard_map/all_gather | solution.py:54
  302.6 20.5 %copy.26 = bf16[192,65536]{1,0:T(8,128)(2,1)} copy(bf16[192,65536]{1,0:T(8,128)(2,1)} %all-gather.2.cloned.1.call-done) | data formatting | bytes 50331648
  (4 shorter events, 0.1 us)
Async XLA Ops:
  7.2 295.5 %all-gather.2.cloned.1.call-start = ((), (), s32[]{:S(2)}) async-start(), calls=%async_computation.1 | async-start | bytes 37748736 | tf_op jit(solution)/shard_map/all_gather | solution.py:54
Sparse Core Ops, SparseCore 0:
  263.3 39.3 all-gather.1
where the time goes:
time: 331 us; the launch traced here: 330 us
  other arithmetic  126 us (38%)
  blocking collectives  75.2 us (23%)
  local copies, waits for them, and re-layouts  74.6 us (23%)
  waiting for transfers between devices  39.5 us (12%)
  between operations  14.8 us (4%)
    all_to_all x2, local copies, waits for them, and re-layouts, device_step(): received = lax.all_to_all(grad_slab, 'data', 1, 0, tiled=True)  53.5 us
    reduce_sum x1, other arithmetic, device_step(): jnp.sum(master * master, axis=1)  52.4 us
    all_gather x1, waiting for transfers between devices, device_step(): lax.all_gather(new_master.astype(jnp.bfloat16), 'data', axis=1, tiled=True)  39.5 us
    convert_element_type x1, other arithmetic, device_step(): new_master.astype(jnp.bfloat16)  37.1 us
    all_to_all x1, blocking collectives, device_step(): received = lax.all_to_all(grad_slab, 'data', 1, 0, tiled=True)  26.7 us
    psum x1, blocking collectives, device_step(): total_sq = lax.psum(jnp.sum(grad_mean * grad_mean), both_axes)  25 us
    reduce_sum x1, other arithmetic, device_step(): jnp.sum(received.reshape(data_size, grad_slab.shape[0], -1), axis=0, dtyp...  23.9 us
    psum x1, blocking collectives, device_step(): lax.psum(jnp.stack([jnp.sum(master * master, axis=1), jnp.sum(direction *...  23.5 us
  transfers between devices with their start and end apart: 1, of which 1 were waited for; matrix products, arithmetic and copies ran while one was open for 0% of the time, Pallas kernels for 0%

commit v1 on v0

v1 whole, which is shorter than its diff:
```python
import functools

import jax
import jax.numpy as jnp
from jax import lax
from jax.experimental import pallas as pl
from jax.experimental.pallas import tpu as pltpu
from jax.sharding import PartitionSpec as P

STEP = 4
LEARN_RATE = 0.08
BETA_ONE = 0.9
BETA_TWO = 0.999
EPSILON = 1e-6
WEIGHT_DECAY = 0.01
MAX_NORM = 1.0
CORR_ONE = 1.0 - BETA_ONE ** STEP
CORR_TWO = 1.0 - BETA_TWO ** STEP
TINY = 1.2e-38

MESH = pl.DeviceIdType.MESH
F32 = jnp.float32
BF16 = jnp.bfloat16
SCOPE = 4000 << 10
LANES = 128
GROUP = 8

PART = 16384
LAND_SLOTS = 8
OWN_SLOTS = 6
RING = 24
LAG = 6
CHUNK = 8192
SEND_SLOTS = 4
WRITE_SLOTS = 6
WRITE_CHUNK = 8192


def rows(group):
    return pl.ds(pl.multiple_of(group * GROUP, GROUP), GROUP)


def lanes_of():
    return lax.broadcasted_iota(jnp.int32, (GROUP, LANES), 1)


def put_lane(tile, lane_ids, lane, partial):
    row_sum = jnp.sum(partial, axis=1, keepdims=True)
    return tile + jnp.where(lane_ids == lane, row_sum, 0.0)


def tree_sum(values):
    while len(values) > 1:
        values = [a + b for a, b in zip(values[::2], values[1::2])] + ([values[-1]] if len(values) % 2 else [])
    return values[0]


def peers(model_size, data_size):
    model, data = lax.axis_index('model'), lax.axis_index('data')
    out = []
    for step in range(1, model_size * data_size):
        peer_model = lax.rem(model + step // data_size, model_size)
        peer_data = lax.rem(data + step % data_size, data_size)
        out.append(((peer_model, peer_data), peer_model * data_size + peer_data))
    return model * data_size + data, out


def enter(others):
    barrier = pltpu.get_barrier_semaphore()
    for device, _ in others:
        pl.semaphore_signal(barrier, inc=1, device_id=device, device_id_type=MESH)
    pl.semaphore_wait(barrier, len(others))


def share(me, others, source, slots, send_sem, recv_sem):
    copies = []
    for device, index in others:
        copy = pltpu.make_async_remote_copy(src_ref=source, dst_ref=slots.at[me], send_sem=send_sem.at[index], recv_sem=recv_sem.at[me], device_id=device, device_id_type=MESH)
        copy.start()
        copies.append(copy)
    for device, index in others:
        pltpu.make_async_remote_copy(src_ref=source, dst_ref=slots.at[index], send_sem=send_sem.at[index], recv_sem=recv_sem.at[index], device_id=device, device_id_type=MESH).wait_recv()
    for copy in copies:
        copy.wait_send()


def exchange_kernel(sizes, groups, cols, grads, master, one_in, two_in, mean_ref, weight_ref, ring, clip_ref, stat_ref, land, own, part, slots,
                    send_sem, recv_sem, free_sem, own_sem, weight_sem, ring_sem, small_send, small_recv):
    model_size, data_size = sizes
    data = lax.axis_index('data')
    me, others = peers(model_size, data_size)
    peer = lax.rem(data + 1, data_size)
    peer_device = (lax.axis_index('model'), peer)
    per_group = cols // PART
    parts = groups * per_group

    def columns(index, base):
        return pl.ds(pl.multiple_of(base + lax.rem(index, per_group) * PART, PART), PART)

    def own_copy(index):
        slot = lax.rem(index, OWN_SLOTS)
        return pltpu.make_async_copy(grads.at[0, rows(index // per_group), columns(index, data * cols)], own.at[slot], own_sem.at[slot])

    def weight_copy(index):
        at = (rows(index // per_group), columns(index, 0))
        return pltpu.make_async_copy(master.at[at], weight_ref.at[at], weight_sem.at[index])

    def send_copy(index):
        slot = lax.rem(index, LAND_SLOTS)
        return pltpu.make_async_remote_copy(src_ref=grads.at[0, rows(index // per_group), columns(index, peer * cols)], dst_ref=land.at[slot],
                                            send_sem=send_sem.at[slot], recv_sem=recv_sem.at[slot], device_id=peer_device, device_id_type=MESH)

    def ring_copies(chunk):
        at = (rows(chunk // (cols // CHUNK)), pl.ds(pl.multiple_of(lax.rem(chunk, cols // CHUNK) * CHUNK, CHUNK), CHUNK))
        return (pltpu.make_async_copy(one_in.at[at], ring.at[0, chunk], ring_sem.at[0, chunk]), pltpu.make_async_copy(two_in.at[at], ring.at[1, chunk], ring_sem.at[1, chunk]))

    for index in range(OWN_SLOTS):
        own_copy(index).start()
        weight_copy(index).start()
    enter(others)
    for index in range(LAND_SLOTS):
        send_copy(index).start()
    lane_ids = lanes_of()
    width = 1024
    zero = jnp.zeros((GROUP, LANES), F32)

    def one_part(index, carry):
        total, stat = carry
        own_slot, land_slot = lax.rem(index, OWN_SLOTS), lax.rem(index, LAND_SLOTS)
        row_at = rows(index // per_group)
        col_at = lax.rem(index, per_group) * PART

        @pl.when(lax.rem(index, parts // RING) == 0)
        def _():
            for copy in ring_copies(index // (parts // RING)):
                copy.start()

        own_copy(index).wait()
        weight_copy(index).wait()
        send_copy(index).wait_recv()

        def piece(step, sums):
            grad_sum, weight_sum = sums
            near = pl.ds(pl.multiple_of(step * width, width), width)
            far = pl.ds(pl.multiple_of(col_at + step * width, width), width)
            mean = (own[own_slot, :, near].astype(F32) + land[land_slot, :, near].astype(F32)) * 0.5
            mean_ref[row_at, far] = mean
            weight = weight_ref[row_at, far]
            cuts = range(0, width, LANES)
            grad_sum += tree_sum([mean[:, at:at + LANES] * mean[:, at:at + LANES] for at in cuts])
            weight_sum += tree_sum([weight[:, at:at + LANES] * weight[:, at:at + LANES] for at in cuts])
            return grad_sum, weight_sum

        grad_sum, weight_sum = lax.fori_loop(0, PART // width, piece, (zero, zero), unroll=2)

        @pl.when(index + LAND_SLOTS < parts)
        def _():
            pl.semaphore_signal(free_sem, inc=1, device_id=peer_device, device_id_type=MESH)

        @pl.when(index + OWN_SLOTS < parts)
        def _():
            own_copy(index + OWN_SLOTS).start()
            weight_copy(index + OWN_SLOTS).start()

        send_copy(index).wait_send()

        @pl.when(index + LAND_SLOTS < parts)
        def _():
            pl.semaphore_wait(free_sem, 1)
            send_copy(index + LAND_SLOTS).start()

        return total + grad_sum, put_lane(stat, lane_ids, index // per_group, weight_sum)

    total, stat = lax.fori_loop(0, parts, one_part, (zero, zero))
    stat_ref[...] = stat
    part[...] = total
    slots[me] = part[...]
    share(me, others, part, slots, small_send, small_recv)
    whole = tree_sum([slots[index] for index in range(model_size * data_size)])
    whole = jnp.sum(jnp.sum(whole, axis=1, keepdims=True), axis=0, keepdims=True)
    whole = jnp.broadcast_to(whole, (GROUP, LANES))
    clip_ref[...] = jnp.minimum(1.0, MAX_NORM / jnp.sqrt(whole))

    def finish(chunk, carry):
        for copy in ring_copies(chunk):
            copy.wait()
        return carry

    lax.fori_loop(0, RING, finish, 0)


def moment_kernel(groups, cols, mean_in, weight_in, ring_in, clip, weight_stat, one_in, two_in, dir_ref, weight_ref, ring, one_out, two_out, stat_ref,
                  one_get, two_get, one_put, two_put):
    per_group = cols // CHUNK
    chunks = groups * per_group
    width = 1024
    lane_ids = lanes_of()

    def place(chunk):
        return rows(chunk // per_group), pl.ds(pl.multiple_of(lax.rem(chunk, per_group) * CHUNK, CHUNK), CHUNK)

    def gets(chunk):
        slot = lax.rem(chunk, RING)
        at = place(chunk)
        return (pltpu.make_async_copy(one_in.at[at], ring.at[0, slot], one_get.at[slot]), pltpu.make_async_copy(two_in.at[at], ring.at[1, slot], two_get.at[slot]))

    def puts(chunk):
        slot = lax.rem(chunk, RING)
        at = place(chunk)
        return (pltpu.make_async_copy(ring.at[0, slot], one_out.at[at], one_put.at[slot]), pltpu.make_async_copy(ring.at[1, slot], two_out.at[at], two_put.at[slot]))

    def start(copies):
        for copy in copies:
            copy.start()

    def wait(copies):
        for copy in copies:
            copy.wait()

    scale = clip[...]
    one_scale = (1.0 - BETA_ONE) * scale
    two_scale = (1.0 - BETA_TWO) * scale * scale
    ratio = CORR_TWO ** 0.5 / CORR_ONE
    floor = EPSILON * CORR_TWO ** 0.5

    def one_chunk(chunk, stat):
        slot = lax.rem(chunk, RING)
        row_at = rows(chunk // per_group)
        col_at = lax.rem(chunk, per_group) * CHUNK

        @pl.when(chunk >= RING)
        def _():
            wait(gets(chunk))

        def piece(index, total):
            squares = []
            for at in range(0, width, LANES):
                near = pl.ds(pl.multiple_of(index * width + at, LANES), LANES)
                far = pl.ds(pl.multiple_of(col_at + index * width + at, LANES), LANES)
                mean = dir_ref[row_at, far]
                new_one = BETA_ONE * ring[0, slot, :, near] + one_scale * mean
                new_two = BETA_TWO * ring[1, slot, :, near] + two_scale * mean * mean
                ring[0, slot, :, near] = new_one
                ring[1, slot, :, near] = new_two
                root = new_two * lax.rsqrt(jnp.maximum(new_two, TINY))
                direction = (new_one * ratio) / (root + floor) + WEIGHT_DECAY * weight_ref[row_at, far]
                dir_ref[row_at, far] = direction
                squares.append(direction * direction)
            return total + tree_sum(squares)

        total = lax.fori_loop(0, CHUNK // width, piece, jnp.zeros((GROUP, LANES), F32))
        start(puts(chunk))
        ahead = chunk + RING - LAG

        @pl.when(jnp.logical_and(ahead >= RING, ahead < chunks))
        def _():
            wait(puts(ahead - RING))
            start(gets(ahead))

        return put_lane(stat, lane_ids, chunk // per_group, total)

    stat_ref[0] = lax.fori_loop(0, chunks, one_chunk, jnp.zeros((GROUP, LANES), F32))
    stat_ref[1] = weight_stat[...]

    def finish(chunk, carry):
        wait(puts(chunk))
        return carry

    lax.fori_loop(chunks - RING, chunks, finish, 0)


def segment_sums(values):
    lane_ids = lanes_of()
    row_ids = lax.broadcasted_iota(jnp.int32, (GROUP, LANES), 0)
    kind = lax.rem(lane_ids, 3)
    first = jnp.where(kind == 0, 3, 4)
    second = jnp.where(kind == 0, 4, jnp.where(kind == 1, 7, 8))
    segment = jnp.where(row_ids < first, 0, jnp.where(row_ids < second, 1, 2))
    out = jnp.zeros((GROUP, LANES), F32)
    for index in range(3):
        inside = segment == index
        out = jnp.where(inside, jnp.sum(jnp.where(inside, values, 0.0), axis=0, keepdims=True), out)
    return out


def weight_kernel(sizes, groups, cols, direction, weight, stats, land, rate, slots, packed, send_sem, recv_sem, small_send, small_recv):
    model_size, data_size = sizes
    data = lax.axis_index('data')
    me, others = peers(model_size, data_size)
    peer_device = (lax.axis_index('model'), lax.rem(data + 1, data_size))
    enter(others)
    slots[me] = stats[...]
    share(me, others, stats, slots, small_send, small_recv)
    lane_ids = lanes_of()
    dir_sq = segment_sums(tree_sum([slots[index, 0] for index in range(model_size * data_size)]))
    weight_sq = segment_sums(tree_sum([slots[index, 1] for index in range(model_size * data_size)]))
    rate[...] = LEARN_RATE * (jnp.sqrt(weight_sq) / jnp.sqrt(dir_sq))
    width = 1024

    def send_copy(group):
        slot = lax.rem(group, SEND_SLOTS)
        return pltpu.make_async_remote_copy(src_ref=packed.at[slot], dst_ref=land.at[group], send_sem=send_sem.at[slot], recv_sem=recv_sem.at[group],
                                            device_id=peer_device, device_id_type=MESH)

    def one_group(group, carry):
        slot = lax.rem(group, SEND_SLOTS)

        @pl.when(group >= SEND_SLOTS)
        def _():
            send_copy(group - SEND_SLOTS).wait_send()

        group_rate = jnp.sum(jnp.where(lane_ids == group, rate[...], 0.0), axis=1, keepdims=True)

        def piece(index, inner):
            at = pl.ds(pl.multiple_of(index * width, width), width)
            packed[slot, :, at] = (weight[rows(group), at] - group_rate * direction[rows(group), at]).astype(BF16)
            return inner

        lax.fori_loop(0, cols // width, piece, 0, unroll=2)
        send_copy(group).start()
        return carry

    lax.fori_loop(0, groups, one_group, 0)

    def finish(group, carry):
        send_copy(group).wait_recv()
        return carry

    lax.fori_loop(0, groups, finish, 0)
    for group in range(groups - SEND_SLOTS, groups):
        send_copy(group).wait_send()


def write_kernel(sizes, groups, cols, direction, weight, land, rate, params, master, fresh, packed, master_sem, land_sem, own_sem):
    data_size = sizes[1]
    data = lax.axis_index('data')
    peer = lax.rem(data + 1, data_size)
    width = 1024
    lane_ids = lanes_of()
    per_group = cols // WRITE_CHUNK
    chunks = groups * per_group

    def columns(chunk, base):
        return pl.ds(pl.multiple_of(base + lax.rem(chunk, per_group) * WRITE_CHUNK, WRITE_CHUNK), WRITE_CHUNK)

    def puts(chunk):
        slot = lax.rem(chunk, WRITE_SLOTS)
        at = rows(chunk // per_group)
        return (pltpu.make_async_copy(fresh.at[slot], master.at[at, columns(chunk, 0)], master_sem.at[slot]),
                pltpu.make_async_copy(packed.at[slot], params.at[at, columns(chunk, data * cols)], own_sem.at[slot]))

    def land_copy(group):
        return pltpu.make_async_copy(land.at[group], params.at[rows(group), pl.ds(pl.multiple_of(peer * cols, LANES), cols)], land_sem.at[group])

    def one_chunk(chunk, carry):
        slot = lax.rem(chunk, WRITE_SLOTS)
        group = chunk // per_group

        @pl.when(lax.rem(chunk, per_group) == 0)
        def _():
            land_copy(group).start()

        @pl.when(chunk >= WRITE_SLOTS)
        def _():
            for copy in puts(chunk - WRITE_SLOTS):
                copy.wait()

        group_rate = jnp.sum(jnp.where(lane_ids == group, rate[...], 0.0), axis=1, keepdims=True)

        def piece(index, inner):
            near = pl.ds(pl.multiple_of(index * width, width), width)
            far = pl.ds(pl.multiple_of(lax.rem(chunk, per_group) * WRITE_CHUNK + index * width, width), width)
            new = weight[rows(group), far] - group_rate * direction[rows(group), far]
            fresh[slot, :, near] = new
            packed[slot, :, near] = new.astype(BF16)
            return inner

        lax.fori_loop(0, WRITE_CHUNK // width, piece, 0, unroll=2)
        for copy in puts(chunk):
            copy.start()
        return carry

    lax.fori_loop(0, chunks, one_chunk, 0)

    def finish(group, carry):
        land_copy(group).wait()
        return carry

    lax.fori_loop(0, groups, finish, 0)
    for chunk in range(chunks - WRITE_SLOTS, chunks):
        for copy in puts(chunk):
            copy.wait()


def solution(mesh):
    sizes = (mesh.shape['model'], mesh.shape['data'])
    devices = sizes[0] * sizes[1]
    both_axes = ('model', 'data')
    state_spec = P(None, both_axes)
    hbm = pl.BlockSpec(memory_space=pl.ANY)
    vmem = pl.BlockSpec(memory_space=pltpu.VMEM)
    dma = pltpu.SemaphoreType.DMA

    def device_step(local_grads, master, moment_one, moment_two):
        blocks, cols = master.shape
        groups = blocks // GROUP
        kept = pltpu.VMEM((blocks, cols), F32)
        keep = functools.partial(pltpu.with_memory_space_constraint, memory_space=pltpu.VMEM)
        tile = jax.ShapeDtypeStruct((GROUP, LANES), F32)
        state = jax.ShapeDtypeStruct((blocks, cols), F32)

        landed = pltpu.VMEM((groups, GROUP, cols), BF16)
        ring_shape = pltpu.VMEM((2, RING, GROUP, CHUNK), F32)
        landed = pltpu.VMEM((groups, GROUP, cols), BF16)
        parts = groups * (cols // PART)

        mean, weight, ring, clip, weight_stat = pl.pallas_call(
            functools.partial(exchange_kernel, sizes, groups, cols),
            out_shape=(kept, kept, ring_shape, tile, tile),
            in_specs=[hbm] * 4,
            out_specs=[vmem] * 5,
            scratch_shapes=[pltpu.VMEM((LAND_SLOTS, GROUP, PART), BF16), pltpu.VMEM((OWN_SLOTS, GROUP, PART), BF16), pltpu.VMEM((GROUP, LANES), F32), pltpu.VMEM((devices, GROUP, LANES), F32),
                            dma((LAND_SLOTS,)), dma((LAND_SLOTS,)), pltpu.SemaphoreType.REGULAR, dma((OWN_SLOTS,)), dma((parts,)), dma((2, RING)), dma((devices,)), dma((devices,))],
            compiler_params=pltpu.CompilerParams(collective_id=0, has_side_effects=True, vmem_limit_bytes=SCOPE),
            name='exchange',
        )(local_grads, master, moment_one, moment_two)

        direction, weight, _, new_one, new_two, stats = pl.pallas_call(
            functools.partial(moment_kernel, groups, cols),
            out_shape=(kept, kept, ring_shape, state, state, jax.ShapeDtypeStruct((2, GROUP, LANES), F32)),
            in_specs=[vmem] * 5 + [hbm] * 2,
            out_specs=[vmem, vmem, vmem, hbm, hbm, vmem],
            input_output_aliases={0: 0, 1: 1, 2: 2},
            scratch_shapes=[dma((RING,))] * 4,
            compiler_params=pltpu.CompilerParams(vmem_limit_bytes=SCOPE),
            name='moments',
        )(mean, weight, ring, clip, weight_stat, moment_one, moment_two)

        land, rate = pl.pallas_call(
            functools.partial(weight_kernel, sizes, groups, cols),
            out_shape=(landed, tile),
            in_specs=[vmem] * 3,
            out_specs=[vmem] * 2,
            scratch_shapes=[pltpu.VMEM((devices, 2, GROUP, LANES), F32), pltpu.VMEM((SEND_SLOTS, GROUP, cols), BF16),
                            dma((SEND_SLOTS,)), dma((groups,)), dma((devices,)), dma((devices,))],
            compiler_params=pltpu.CompilerParams(collective_id=1, has_side_effects=True, vmem_limit_bytes=SCOPE),
            name='weights',
        )(keep(direction), keep(weight), stats)

        params, new_master = pl.pallas_call(
            functools.partial(write_kernel, sizes, groups, cols),
            out_shape=(jax.ShapeDtypeStruct((blocks, sizes[1] * cols), BF16), state),
            in_specs=[vmem] * 4,
            out_specs=[hbm, hbm],
            scratch_shapes=[pltpu.VMEM((WRITE_SLOTS, GROUP, WRITE_CHUNK), F32), pltpu.VMEM((WRITE_SLOTS, GROUP, WRITE_CHUNK), BF16),
                            dma((WRITE_SLOTS,)), dma((groups,)), dma((WRITE_SLOTS,))],
            compiler_params=pltpu.CompilerParams(vmem_limit_bytes=SCOPE),
            name='write',
        )(keep(direction), keep(weight), keep(land), rate)
        return params, new_master, new_one, new_two

    return jax.shard_map(device_step, mesh=mesh, in_specs=(P('data', None, 'model'), state_spec, state_spec, state_spec),
                         out_specs=(P(None, 'model'), state_spec, state_spec, state_spec), check_vma=False)
```

time: 331 us -> 225 us (0.68)
  Pallas kernels: 0 us -> 224 us
  other arithmetic: 126 us -> 0 us
  blocking collectives: 75.2 us -> 0 us
  local copies, waits for them, and re-layouts: 74.6 us -> 0 us
  waiting for transfers between devices: 39.5 us -> 0 us
  between operations: 14.8 us -> 0.65 us
    pallas_call x0 -> x4, Pallas kernels: none -> 224 us  [the longest x1 147 us: device_step(): pl.pallas_call(functools.partial(moment_kernel, groups, cols), out_shape=...]
    reduce_sum x5 -> x0, other arithmetic: 88.7 us -> none  [the longest x1 52.4 us: device_step(): jnp.sum(master * master, axis=1)]
    all_to_all x2 -> x0, local copies, waits for them, and re-layouts: 53.5 us -> none  [device_step(): received = lax.all_to_all(grad_slab, 'data', 1, 0, tiled=True)]
    psum x2 -> x0, blocking collectives: 48.5 us -> none  [the longest x1 25 us: device_step(): total_sq = lax.psum(jnp.sum(grad_mean * grad_mean), both_axes)]
    all_gather x1 -> x0, waiting for transfers between devices: 39.5 us -> none  [device_step(): lax.all_gather(new_master.astype(jnp.bfloat16), 'data', axis=1, tiled=True)]
    convert_element_type x1 -> x0, other arithmetic: 37.1 us -> none  [device_step(): new_master.astype(jnp.bfloat16)]
    all_to_all x1 -> x0, blocking collectives: 26.7 us -> none  [device_step(): received = lax.all_to_all(grad_slab, 'data', 1, 0, tiled=True)]
    unnamed x1 -> x0, local copies, waits for them, and re-layouts: 20.5 us -> none
  transfers between devices with their start and end apart: 1 -> 0, of which waited for: 1 -> 0; matrix products, arithmetic and copies ran while one was open for 0% -> 0% of each run, Pallas kernels for 0% -> 0%
where the time goes in v1:
time: 225 us
  Pallas kernels  224 us (100%)
    pallas_call x1, Pallas kernels, device_step(): pl.pallas_call(functools.partial(moment_kernel, groups, cols), out_shape=...  147 us
    pallas_call x1, Pallas kernels, device_step(): pl.pallas_call(functools.partial(exchange_kernel, sizes, groups, cols), o...  34.5 us
    pallas_call x1, Pallas kernels, device_step(): pl.pallas_call(functools.partial(weight_kernel, sizes, groups, cols), out...  25.6 us
    pallas_call x1, Pallas kernels, device_step(): pl.pallas_call(functools.partial(write_kernel, sizes, groups, cols), out_...  17.1 us

profile of v1, /device:TPU:0, one launch (start us, length us, event | category | flops | bytes accessed | tf_op | source)
XLA Modules:
  0.0 225.0 jit_solution(15171193198419006930)
XLA Ops:
  0.6 34.5 %exchange.1 = (f32[192,32768]{1,0:T(8,128)S(1)}, f32[192,32768]{1,0:T(8,128)S(1)}, f32[2,24,8,8192]{3,2,1,0:T(8,128)S(1)}, f32[8,128]{1,0:T(8,128)}, f32[8,128]{1,0:T(8,128)}) custom-call(bf16[1,192,65536]{2,1,0:T(8,128)(2,1)} %grads.1, f32[192,32768]{1,0:T(8,128)} %master.1, f32[192,32768]{1,0:T(8,128)} %one_in.3, f32[192,32768]{1,0:T(8,128)} %two_in.3), custom_call_target="tpu_custom_call" | custom-call | tf_op jit(solution)/shard_map/exchange/pallas_call | solution.py:417
  35.1 147.2 %moments.1 = (f32[192,32768]{1,0:T(8,128)S(1)}, f32[192,32768]{1,0:T(8,128)S(1)}, f32[2,24,8,8192]{3,2,1,0:T(8,128)S(1)}, f32[192,32768]{1,0:T(8,128)}, f32[192,32768]{1,0:T(8,128)}, /*index=5*/f32[2,8,128]{2,1,0:T(8,128)}) custom-call(f32[192,32768]{1,0:T(8,128)S(1)} %get-tuple-element.18.mean_in, ...), custom_call_target="tpu_custom_call", output_to_operand_aliasing={{0}: (0, {}), {1}: (1, {}), {2}: (2, {})} | custom-call | tf_op jit(solution)/shard_map/moments/pallas_call | solution.py:428
  182.2 25.6 %weights.1 = (bf16[24,8,32768]{2,1,0:T(8,128)(2,1)S(1)}, f32[8,128]{1,0:T(8,128)}) custom-call(f32[192,32768]{1,0:T(8,128)S(1)} %get-tuple-element.23.direction, f32[192,32768]{1,0:T(8,128)S(1)} %get-tuple-element.24.weight, f32[2,8,128]{2,1,0:T(8,128)} %get-tuple-element.25.stats), custom_call_target="tpu_custom_call" | custom-call | tf_op jit(solution)/shard_map/weights/pallas_call | solution.py:439
  207.8 17.1 %write.1 = (bf16[192,65536]{1,0:T(8,128)(2,1)}, f32[192,32768]{1,0:T(8,128)}) custom-call(f32[192,32768]{1,0:T(8,128)S(1)} %get-tuple-element.23.direction, f32[192,32768]{1,0:T(8,128)S(1)} %get-tuple-element.24.weight, bf16[24,8,32768]{2,1,0:T(8,128)(2,1)S(1)} %get-tuple-element.26.land, f32[8,128]{1,0:T(8,128)} %get-tuple-element.27.rate), custom_call_target="tpu_custom_call" | custom-call | tf_op jit(solution)/shard_map/write/pallas_call | solution.py:450

commit v2 on v1

--- a/solution.py
+++ b/solution.py
@@ -30,6 +30,8 @@
 OWN_SLOTS = 6
 RING = 24
 LAG = 6
+MOMENT_WIDTH = 2048
+MEAN_WIDTH = 2048
 CHUNK = 8192
 SEND_SLOTS = 4
 WRITE_SLOTS = 6
@@ -121,7 +123,7 @@
     for index in range(LAND_SLOTS):
         send_copy(index).start()
     lane_ids = lanes_of()
-    width = 1024
+    width = MEAN_WIDTH
     zero = jnp.zeros((GROUP, LANES), F32)
 
     def one_part(index, carry):
@@ -143,15 +145,15 @@
             grad_sum, weight_sum = sums
             near = pl.ds(pl.multiple_of(step * width, width), width)
             far = pl.ds(pl.multiple_of(col_at + step * width, width), width)
+            weight = weight_ref[row_at, far]
             mean = (own[own_slot, :, near].astype(F32) + land[land_slot, :, near].astype(F32)) * 0.5
             mean_ref[row_at, far] = mean
-            weight = weight_ref[row_at, far]
             cuts = range(0, width, LANES)
             grad_sum += tree_sum([mean[:, at:at + LANES] * mean[:, at:at + LANES] for at in cuts])
             weight_sum += tree_sum([weight[:, at:at + LANES] * weight[:, at:at + LANES] for at in cuts])
             return grad_sum, weight_sum
 
-        grad_sum, weight_sum = lax.fori_loop(0, PART // width, piece, (zero, zero), unroll=2)
+        grad_sum, weight_sum = lax.fori_loop(0, PART // width, piece, (zero, zero))
 
         @pl.when(index + LAND_SLOTS < parts)
         def _():
@@ -193,7 +195,7 @@
                   one_get, two_get, one_put, two_put):
     per_group = cols // CHUNK
     chunks = groups * per_group
-    width = 1024
+    width = MOMENT_WIDTH
     lane_ids = lanes_of()
 
     def place(chunk):
@@ -217,7 +219,7 @@
         for copy in copies:
             copy.wait()
 
-    scale = clip[...]
+    scale = jnp.concatenate([clip[...]] * (width // LANES), axis=1)
     one_scale = (1.0 - BETA_ONE) * scale
     two_scale = (1.0 - BETA_TWO) * scale * scale
     ratio = CORR_TWO ** 0.5 / CORR_ONE
@@ -233,20 +235,18 @@
             wait(gets(chunk))
 
         def piece(index, total):
-            squares = []
-            for at in range(0, width, LANES):
-                near = pl.ds(pl.multiple_of(index * width + at, LANES), LANES)
-                far = pl.ds(pl.multiple_of(col_at + index * width + at, LANES), LANES)
-                mean = dir_ref[row_at, far]
-                new_one = BETA_ONE * ring[0, slot, :, near] + one_scale * mean
-                new_two = BETA_TWO * ring[1, slot, :, near] + two_scale * mean * mean
-                ring[0, slot, :, near] = new_one
-                ring[1, slot, :, near] = new_two
-                root = new_two * lax.rsqrt(jnp.maximum(new_two, TINY))
-                direction = (new_one * ratio) / (root + floor) + WEIGHT_DECAY * weight_ref[row_at, far]
-                dir_ref[row_at, far] = direction
-                squares.append(direction * direction)
-            return total + tree_sum(squares)
+            near = pl.ds(pl.multiple_of(index * width, width), width)
+            far = pl.ds(pl.multiple_of(col_at + index * width, width), width)
+            mean, weight = dir_ref[row_at, far], weight_ref[row_at, far]
+            old_one, old_two = ring[0, slot, :, near], ring[1, slot, :, near]
+            new_one = BETA_ONE * old_one + one_scale * mean
+            new_two = BETA_TWO * old_two + two_scale * mean * mean
+            root = new_two * lax.rsqrt(jnp.maximum(new_two, TINY))
+            direction = (new_one * ratio) / (root + floor) + WEIGHT_DECAY * weight
+            ring[0, slot, :, near] = new_one
+            ring[1, slot, :, near] = new_two
+            dir_ref[row_at, far] = direction
+            return total + tree_sum([direction[:, at:at + LANES] * direction[:, at:at + LANES] for at in range(0, width, LANES)])
 
         total = lax.fori_loop(0, CHUNK // width, piece, jnp.zeros((GROUP, LANES), F32))
         start(puts(chunk))

time: 225 us -> 110 us (0.49)
  Pallas kernels: 224 us -> 109 us
    pallas_call x1, Pallas kernels: 147 us -> 31.7 us  [device_step(): pl.pallas_call(functools.partial(moment_kernel, groups, cols), out_shape=...]
where the time goes in v2:
time: 110 us; the launch traced here: 109 us
  Pallas kernels  109 us (99%)
    pallas_call x1, Pallas kernels, device_step(): pl.pallas_call(functools.partial(exchange_kernel, sizes, groups, cols), o...  34.4 us
    pallas_call x1, Pallas kernels, device_step(): pl.pallas_call(functools.partial(moment_kernel, groups, cols), out_shape=...  31.7 us
    pallas_call x1, Pallas kernels, device_step(): pl.pallas_call(functools.partial(weight_kernel, sizes, groups, cols), out...  25.6 us
    pallas_call x1, Pallas kernels, device_step(): pl.pallas_call(functools.partial(write_kernel, sizes, groups, cols), out_...  17.1 us

profile of v2, /device:TPU:0, one launch (start us, length us, event | category | flops | bytes accessed | tf_op | source)
XLA Modules:
  0.0 109.4 jit_solution(3420594646029700535)
XLA Ops:
  0.6 34.4 %exchange.1 = (f32[192,32768]{1,0:T(8,128)S(1)}, f32[192,32768]{1,0:T(8,128)S(1)}, f32[2,24,8,8192]{3,2,1,0:T(8,128)S(1)}, f32[8,128]{1,0:T(8,128)}, f32[8,128]{1,0:T(8,128)}) custom-call(bf16[1,192,65536]{2,1,0:T(8,128)(2,1)} %grads.1, f32[192,32768]{1,0:T(8,128)} %master.1, f32[192,32768]{1,0:T(8,128)} %one_in.3, f32[192,32768]{1,0:T(8,128)} %two_in.3), custom_call_target="tpu_custom_call" | custom-call | tf_op jit(solution)/shard_map/exchange/pallas_call | solution.py:417
  35.1 31.7 %moments.1 = (f32[192,32768]{1,0:T(8,128)S(1)}, f32[192,32768]{1,0:T(8,128)S(1)}, f32[2,24,8,8192]{3,2,1,0:T(8,128)S(1)}, f32[192,32768]{1,0:T(8,128)}, f32[192,32768]{1,0:T(8,128)}, /*index=5*/f32[2,8,128]{2,1,0:T(8,128)}) custom-call(f32[192,32768]{1,0:T(8,128)S(1)} %get-tuple-element.18.mean_in, ...), custom_call_target="tpu_custom_call", output_to_operand_aliasing={{0}: (0, {}), {1}: (1, {}), {2}: (2, {})} | custom-call | tf_op jit(solution)/shard_map/moments/pallas_call | solution.py:428
  66.7 25.6 %weights.1 = (bf16[24,8,32768]{2,1,0:T(8,128)(2,1)S(1)}, f32[8,128]{1,0:T(8,128)}) custom-call(f32[192,32768]{1,0:T(8,128)S(1)} %get-tuple-element.23.direction, f32[192,32768]{1,0:T(8,128)S(1)} %get-tuple-element.24.weight, f32[2,8,128]{2,1,0:T(8,128)} %get-tuple-element.25.stats), custom_call_target="tpu_custom_call" | custom-call | tf_op jit(solution)/shard_map/weights/pallas_call | solution.py:439
  92.3 17.1 %write.1 = (bf16[192,65536]{1,0:T(8,128)(2,1)}, f32[192,32768]{1,0:T(8,128)}) custom-call(f32[192,32768]{1,0:T(8,128)S(1)} %get-tuple-element.23.direction, f32[192,32768]{1,0:T(8,128)S(1)} %get-tuple-element.24.weight, bf16[24,8,32768]{2,1,0:T(8,128)(2,1)S(1)} %get-tuple-element.26.land, f32[8,128]{1,0:T(8,128)} %get-tuple-element.27.rate), custom_call_target="tpu_custom_call" | custom-call | tf_op jit(solution)/shard_map/write/pallas_call | solution.py:450

commit v3 on v2

--- a/solution.py
+++ b/solution.py
@@ -26,15 +26,16 @@
 GROUP = 8
 
 PART = 16384
-LAND_SLOTS = 8
-OWN_SLOTS = 6
+LAND_SLOTS = 11
+OWN_SLOTS = 4
+EARLY = 16
 RING = 24
-LAG = 6
+LAG = 8
 MOMENT_WIDTH = 2048
 MEAN_WIDTH = 2048
 CHUNK = 8192
 SEND_SLOTS = 4
-WRITE_SLOTS = 6
+WRITE_SLOTS = 10
 WRITE_CHUNK = 8192
 
 
@@ -118,10 +119,11 @@
 
     for index in range(OWN_SLOTS):
         own_copy(index).start()
-        weight_copy(index).start()
     enter(others)
     for index in range(LAND_SLOTS):
         send_copy(index).start()
+    for index in range(OWN_SLOTS):
+        weight_copy(index).start()
     lane_ids = lanes_of()
     width = MEAN_WIDTH
     zero = jnp.zeros((GROUP, LANES), F32)
@@ -132,9 +134,9 @@
         row_at = rows(index // per_group)
         col_at = lax.rem(index, per_group) * PART
 
-        @pl.when(lax.rem(index, parts // RING) == 0)
-        def _():
-            for copy in ring_copies(index // (parts // RING)):
+        @pl.when(lax.rem(index, parts // EARLY) == 0)
+        def _():
+            for copy in ring_copies(index // (parts // EARLY)):
                 copy.start()
 
         own_copy(index).wait()
@@ -188,7 +190,7 @@
             copy.wait()
         return carry
 
-    lax.fori_loop(0, RING, finish, 0)
+    lax.fori_loop(0, EARLY, finish, 0)
 
 
 def moment_kernel(groups, cols, mean_in, weight_in, ring_in, clip, weight_stat, one_in, two_in, dir_ref, weight_ref, ring, one_out, two_out, stat_ref,
@@ -211,9 +213,9 @@
         at = place(chunk)
         return (pltpu.make_async_copy(ring.at[0, slot], one_out.at[at], one_put.at[slot]), pltpu.make_async_copy(ring.at[1, slot], two_out.at[at], two_put.at[slot]))
 
-    def start(copies):
+    def start(copies, priority=0):
         for copy in copies:
-            copy.start()
+            copy.start(priority=priority)
 
     def wait(copies):
         for copy in copies:
@@ -225,12 +227,18 @@
     ratio = CORR_TWO ** 0.5 / CORR_ONE
     floor = EPSILON * CORR_TWO ** 0.5
 
+    def begin(chunk, carry):
+        start(gets(chunk))
+        return carry
+
+    lax.fori_loop(EARLY, RING - LAG, begin, 0)
+
     def one_chunk(chunk, stat):
         slot = lax.rem(chunk, RING)
         row_at = rows(chunk // per_group)
         col_at = lax.rem(chunk, per_group) * CHUNK
 
-        @pl.when(chunk >= RING)
+        @pl.when(chunk >= EARLY)
         def _():
             wait(gets(chunk))
 
@@ -249,12 +257,15 @@
             return total + tree_sum([direction[:, at:at + LANES] * direction[:, at:at + LANES] for at in range(0, width, LANES)])
 
         total = lax.fori_loop(0, CHUNK // width, piece, jnp.zeros((GROUP, LANES), F32))
-        start(puts(chunk))
+        start(puts(chunk), priority=1)
         ahead = chunk + RING - LAG
 
         @pl.when(jnp.logical_and(ahead >= RING, ahead < chunks))
         def _():
             wait(puts(ahead - RING))
+
+        @pl.when(ahead < chunks)
+        def _():
             start(gets(ahead))
 
         return put_lane(stat, lane_ids, chunk // per_group, total)
@@ -356,10 +367,6 @@
         slot = lax.rem(chunk, WRITE_SLOTS)
         group = chunk // per_group
 
-        @pl.when(lax.rem(chunk, per_group) == 0)
-        def _():
-            land_copy(group).start()
-
         @pl.when(chunk >= WRITE_SLOTS)
         def _():
             for copy in puts(chunk - WRITE_SLOTS):
@@ -380,6 +387,11 @@
             copy.start()
         return carry
 
+    def begin(group, carry):
+        land_copy(group).start(priority=1)
+        return carry
+
+    lax.fori_loop(0, groups, begin, 0)
     lax.fori_loop(0, chunks, one_chunk, 0)
 
     def finish(group, carry):
@@ -420,7 +432,7 @@
             in_specs=[hbm] * 4,
             out_specs=[vmem] * 5,
             scratch_shapes=[pltpu.VMEM((LAND_SLOTS, GROUP, PART), BF16), pltpu.VMEM((OWN_SLOTS, GROUP, PART), BF16), pltpu.VMEM((GROUP, LANES), F32), pltpu.VMEM((devices, GROUP, LANES), F32),
-                            dma((LAND_SLOTS,)), dma((LAND_SLOTS,)), pltpu.SemaphoreType.REGULAR, dma((OWN_SLOTS,)), dma((parts,)), dma((2, RING)), dma((devices,)), dma((devices,))],
+                            dma((LAND_SLOTS,)), dma((LAND_SLOTS,)), pltpu.SemaphoreType.REGULAR, dma((OWN_SLOTS,)), dma((parts,)), dma((2, EARLY)), dma((devices,)), dma((devices,))],
             compiler_params=pltpu.CompilerParams(collective_id=0, has_side_effects=True, vmem_limit_bytes=SCOPE),
             name='exchange',
         )(local_grads, master, moment_one, moment_two)

time: 110 us -> 111 us (level)
  no operation moved by 1% of the time
where the time goes in v3:
time: 111 us
  Pallas kernels  110 us (99%)
    pallas_call x1, Pallas kernels, device_step(): pl.pallas_call(functools.partial(exchange_kernel, sizes, groups, cols), o...  34.7 us
    pallas_call x1, Pallas kernels, device_step(): pl.pallas_call(functools.partial(moment_kernel, groups, cols), out_shape=...  32.4 us
    pallas_call x1, Pallas kernels, device_step(): pl.pallas_call(functools.partial(weight_kernel, sizes, groups, cols), out...  25.6 us
    pallas_call x1, Pallas kernels, device_step(): pl.pallas_call(functools.partial(write_kernel, sizes, groups, cols), out_...  17.7 us

profile of v3, /device:TPU:0, one launch (start us, length us, event | category | flops | bytes accessed | tf_op | source)
XLA Modules:
  0.0 111.0 jit_solution(3438994740826975440)
XLA Ops:
  0.6 34.7 %exchange.1 = (f32[192,32768]{1,0:T(8,128)S(1)}, f32[192,32768]{1,0:T(8,128)S(1)}, f32[2,24,8,8192]{3,2,1,0:T(8,128)S(1)}, f32[8,128]{1,0:T(8,128)}, f32[8,128]{1,0:T(8,128)}) custom-call(bf16[1,192,65536]{2,1,0:T(8,128)(2,1)} %grads.1, f32[192,32768]{1,0:T(8,128)} %master.1, f32[192,32768]{1,0:T(8,128)} %one_in.3, f32[192,32768]{1,0:T(8,128)} %two_in.3), custom_call_target="tpu_custom_call" | custom-call | tf_op jit(solution)/shard_map/exchange/pallas_call | solution.py:429
  35.3 32.4 %moments.1 = (f32[192,32768]{1,0:T(8,128)S(1)}, f32[192,32768]{1,0:T(8,128)S(1)}, f32[2,24,8,8192]{3,2,1,0:T(8,128)S(1)}, f32[192,32768]{1,0:T(8,128)}, f32[192,32768]{1,0:T(8,128)}, /*index=5*/f32[2,8,128]{2,1,0:T(8,128)}) custom-call(f32[192,32768]{1,0:T(8,128)S(1)} %get-tuple-element.18.mean_in, ...), custom_call_target="tpu_custom_call", output_to_operand_aliasing={{0}: (0, {}), {1}: (1, {}), {2}: (2, {})} | custom-call | tf_op jit(solution)/shard_map/moments/pallas_call | solution.py:440
  67.7 25.6 %weights.1 = (bf16[24,8,32768]{2,1,0:T(8,128)(2,1)S(1)}, f32[8,128]{1,0:T(8,128)}) custom-call(f32[192,32768]{1,0:T(8,128)S(1)} %get-tuple-element.23.direction, f32[192,32768]{1,0:T(8,128)S(1)} %get-tuple-element.24.weight, f32[2,8,128]{2,1,0:T(8,128)} %get-tuple-element.25.stats), custom_call_target="tpu_custom_call" | custom-call | tf_op jit(solution)/shard_map/weights/pallas_call | solution.py:451
  93.3 17.7 %write.1 = (bf16[192,65536]{1,0:T(8,128)(2,1)}, f32[192,32768]{1,0:T(8,128)}) custom-call(f32[192,32768]{1,0:T(8,128)S(1)} %get-tuple-element.23.direction, f32[192,32768]{1,0:T(8,128)S(1)} %get-tuple-element.24.weight, bf16[24,8,32768]{2,1,0:T(8,128)(2,1)S(1)} %get-tuple-element.26.land, f32[8,128]{1,0:T(8,128)} %get-tuple-element.27.rate), custom_call_target="tpu_custom_call" | custom-call | tf_op jit(solution)/shard_map/write/pallas_call | solution.py:462

commit v4 on v2

--- a/solution.py
+++ b/solution.py
@@ -26,16 +26,18 @@
 GROUP = 8
 
 PART = 16384
+AHEAD = 4
 LAND_SLOTS = 8
+STAGE_SLOTS = 9
 OWN_SLOTS = 6
-RING = 24
-LAG = 6
+RING = 20
+LAG = 7
 MOMENT_WIDTH = 2048
 MEAN_WIDTH = 2048
 CHUNK = 8192
 SEND_SLOTS = 4
-WRITE_SLOTS = 6
-WRITE_CHUNK = 8192
+WRITE_SLOTS = 5
+WRITE_CHUNK = 16384
 
 
 def rows(group):
@@ -86,8 +88,8 @@
         copy.wait_send()
 
 
-def exchange_kernel(sizes, groups, cols, grads, master, one_in, two_in, mean_ref, weight_ref, ring, clip_ref, stat_ref, land, own, part, slots,
-                    send_sem, recv_sem, free_sem, own_sem, weight_sem, ring_sem, small_send, small_recv):
+def exchange_kernel(sizes, groups, cols, grads, master, one_in, two_in, mean_ref, weight_ref, ring, land, clip_ref, stat_ref, stage, own, part, slots,
+                    stage_sem, send_sem, recv_sem, free_sem, own_sem, weight_sem, ring_sem, small_send, small_recv):
     model_size, data_size = sizes
     data = lax.axis_index('data')
     me, others = peers(model_size, data_size)
@@ -107,24 +109,41 @@
         at = (rows(index // per_group), columns(index, 0))
         return pltpu.make_async_copy(master.at[at], weight_ref.at[at], weight_sem.at[index])
 
+    def stage_copy(index):
+        slot = lax.rem(index, STAGE_SLOTS)
+        return pltpu.make_async_copy(grads.at[0, rows(index // per_group), columns(index, peer * cols)], stage.at[slot], stage_sem.at[slot])
+
     def send_copy(index):
-        slot = lax.rem(index, LAND_SLOTS)
-        return pltpu.make_async_remote_copy(src_ref=grads.at[0, rows(index // per_group), columns(index, peer * cols)], dst_ref=land.at[slot],
-                                            send_sem=send_sem.at[slot], recv_sem=recv_sem.at[slot], device_id=peer_device, device_id_type=MESH)
+        from_slot, to_slot = lax.rem(index, STAGE_SLOTS), lax.rem(index, LAND_SLOTS)
+        return pltpu.make_async_remote_copy(src_ref=stage.at[from_slot], dst_ref=land.at[to_slot], send_sem=send_sem.at[from_slot], recv_sem=recv_sem.at[to_slot],
+                                            device_id=peer_device, device_id_type=MESH)
 
     def ring_copies(chunk):
         at = (rows(chunk // (cols // CHUNK)), pl.ds(pl.multiple_of(lax.rem(chunk, cols // CHUNK) * CHUNK, CHUNK), CHUNK))
         return (pltpu.make_async_copy(one_in.at[at], ring.at[0, chunk], ring_sem.at[0, chunk]), pltpu.make_async_copy(two_in.at[at], ring.at[1, chunk], ring_sem.at[1, chunk]))
 
-    for index in range(OWN_SLOTS):
+    def begin_stage(index, carry):
+        stage_copy(index).start()
+        return carry
+
+    def begin_own(index, carry):
         own_copy(index).start()
         weight_copy(index).start()
+        return carry
+
+    def begin_send(index, carry):
+        stage_copy(index).wait()
+        send_copy(index).start()
+        return carry
+
+    lax.fori_loop(0, STAGE_SLOTS, begin_stage, 0)
+    lax.fori_loop(0, OWN_SLOTS, begin_own, 0)
     enter(others)
-    for index in range(LAND_SLOTS):
-        send_copy(index).start()
+    lax.fori_loop(0, AHEAD, begin_send, 0)
     lane_ids = lanes_of()
     width = MEAN_WIDTH
     zero = jnp.zeros((GROUP, LANES), F32)
+    first_ring = parts - RING // 2
 
     def one_part(index, carry):
         total, stat = carry
@@ -132,10 +151,13 @@
         row_at = rows(index // per_group)
         col_at = lax.rem(index, per_group) * PART
 
-        @pl.when(lax.rem(index, parts // RING) == 0)
-        def _():
-            for copy in ring_copies(index // (parts // RING)):
-                copy.start()
+        @pl.when(jnp.logical_and(index + AHEAD >= LAND_SLOTS, index + AHEAD < parts))
+        def _():
+            pl.semaphore_wait(free_sem, 1)
+
+        @pl.when(index + AHEAD < parts)
+        def _():
+            begin_send(index + AHEAD, 0)
 
         own_copy(index).wait()
         weight_copy(index).wait()
@@ -161,15 +183,19 @@
 
         @pl.when(index + OWN_SLOTS < parts)
         def _():
-            own_copy(index + OWN_SLOTS).start()
-            weight_copy(index + OWN_SLOTS).start()
+            begin_own(index + OWN_SLOTS, 0)
 
         send_copy(index).wait_send()
 
-        @pl.when(index + LAND_SLOTS < parts)
-        def _():
-            pl.semaphore_wait(free_sem, 1)
-            send_copy(index + LAND_SLOTS).start()
+        @pl.when(index + STAGE_SLOTS < parts)
+        def _():
+            begin_stage(index + STAGE_SLOTS, 0)
+
+        @pl.when(index >= first_ring)
+        def _():
+            for late in range(2):
+                for copy in ring_copies((index - first_ring) * 2 + late):
+                    copy.start()
 
         return total + grad_sum, put_lane(stat, lane_ids, index // per_group, weight_sum)
 
@@ -191,7 +217,7 @@
     lax.fori_loop(0, RING, finish, 0)
 
 
-def moment_kernel(groups, cols, mean_in, weight_in, ring_in, clip, weight_stat, one_in, two_in, dir_ref, weight_ref, ring, one_out, two_out, stat_ref,
+def moment_kernel(groups, cols, mean_in, weight_in, ring_in, land_in, clip, weight_stat, one_in, two_in, dir_ref, weight_ref, ring, land, one_out, two_out, stat_ref,
                   one_get, two_get, one_put, two_put):
     per_group = cols // CHUNK
     chunks = groups * per_group
@@ -211,9 +237,9 @@
         at = place(chunk)
         return (pltpu.make_async_copy(ring.at[0, slot], one_out.at[at], one_put.at[slot]), pltpu.make_async_copy(ring.at[1, slot], two_out.at[at], two_put.at[slot]))
 
-    def start(copies):
+    def start(copies, priority=0):
         for copy in copies:
-            copy.start()
+            copy.start(priority=priority)
 
     def wait(copies):
         for copy in copies:
@@ -249,7 +275,7 @@
             return total + tree_sum([direction[:, at:at + LANES] * direction[:, at:at + LANES] for at in range(0, width, LANES)])
 
         total = lax.fori_loop(0, CHUNK // width, piece, jnp.zeros((GROUP, LANES), F32))
-        start(puts(chunk))
+        start(puts(chunk), priority=1)
         ahead = chunk + RING - LAG
 
         @pl.when(jnp.logical_and(ahead >= RING, ahead < chunks))
@@ -414,27 +440,29 @@
         landed = pltpu.VMEM((groups, GROUP, cols), BF16)
         parts = groups * (cols // PART)
 
-        mean, weight, ring, clip, weight_stat = pl.pallas_call(
+        caught = pltpu.VMEM((LAND_SLOTS, GROUP, PART), BF16)
+
+        mean, weight, ring, catch, clip, weight_stat = pl.pallas_call(
             functools.partial(exchange_kernel, sizes, groups, cols),
-            out_shape=(kept, kept, ring_shape, tile, tile),
+            out_shape=(kept, kept, ring_shape, caught, tile, tile),
             in_specs=[hbm] * 4,
-            out_specs=[vmem] * 5,
-            scratch_shapes=[pltpu.VMEM((LAND_SLOTS, GROUP, PART), BF16), pltpu.VMEM((OWN_SLOTS, GROUP, PART), BF16), pltpu.VMEM((GROUP, LANES), F32), pltpu.VMEM((devices, GROUP, LANES), F32),
-                            dma((LAND_SLOTS,)), dma((LAND_SLOTS,)), pltpu.SemaphoreType.REGULAR, dma((OWN_SLOTS,)), dma((parts,)), dma((2, RING)), dma((devices,)), dma((devices,))],
+            out_specs=[vmem] * 6,
+            scratch_shapes=[pltpu.VMEM((STAGE_SLOTS, GROUP, PART), BF16), pltpu.VMEM((OWN_SLOTS, GROUP, PART), BF16), pltpu.VMEM((GROUP, LANES), F32), pltpu.VMEM((devices, GROUP, LANES), F32),
+                            dma((STAGE_SLOTS,)), dma((STAGE_SLOTS,)), dma((LAND_SLOTS,)), pltpu.SemaphoreType.REGULAR, dma((OWN_SLOTS,)), dma((parts,)), dma((2, RING)), dma((devices,)), dma((devices,))],
             compiler_params=pltpu.CompilerParams(collective_id=0, has_side_effects=True, vmem_limit_bytes=SCOPE),
             name='exchange',
         )(local_grads, master, moment_one, moment_two)
 
-        direction, weight, _, new_one, new_two, stats = pl.pallas_call(
+        direction, weight, _, _, new_one, new_two, stats = pl.pallas_call(
             functools.partial(moment_kernel, groups, cols),
-            out_shape=(kept, kept, ring_shape, state, state, jax.ShapeDtypeStruct((2, GROUP, LANES), F32)),
-            in_specs=[vmem] * 5 + [hbm] * 2,
-            out_specs=[vmem, vmem, vmem, hbm, hbm, vmem],
-            input_output_aliases={0: 0, 1: 1, 2: 2},
+            out_shape=(kept, kept, ring_shape, caught, state, state, jax.ShapeDtypeStruct((2, GROUP, LANES), F32)),
+            in_specs=[vmem] * 6 + [hbm] * 2,
+            out_specs=[vmem, vmem, vmem, vmem, hbm, hbm, vmem],
+            input_output_aliases={0: 0, 1: 1, 2: 2, 3: 3},
             scratch_shapes=[dma((RING,))] * 4,
             compiler_params=pltpu.CompilerParams(vmem_limit_bytes=SCOPE),
             name='moments',
-        )(mean, weight, ring, clip, weight_stat, moment_one, moment_two)
+        )(mean, weight, ring, catch, clip, weight_stat, moment_one, moment_two)
 
         land, rate = pl.pallas_call(
             functools.partial(weight_kernel, sizes, groups, cols),

time: 110 us -> 104 us (0.945)
  Pallas kernels: 109 us -> 103 us
    pallas_call x1, Pallas kernels: 34.4 us -> 28 us  [device_step(): pl.pallas_call(functools.partial(exchange_kernel, sizes, groups, cols), o...]
where the time goes in v4:
time: 104 us; the launch traced here: 103 us
  Pallas kernels  103 us (99%)
    pallas_call x1, Pallas kernels, device_step(): pl.pallas_call(functools.partial(moment_kernel, groups, cols), out_shape=...  32.3 us
    pallas_call x1, Pallas kernels, device_step(): pl.pallas_call(functools.partial(exchange_kernel, sizes, groups, cols), o...  28 us
    pallas_call x1, Pallas kernels, device_step(): pl.pallas_call(functools.partial(weight_kernel, sizes, groups, cols), out...  25.6 us
    pallas_call x1, Pallas kernels, device_step(): pl.pallas_call(functools.partial(write_kernel, sizes, groups, cols), out_...  16.8 us

profile of v4, /device:TPU:0, one launch (start us, length us, event | category | flops | bytes accessed | tf_op | source)
XLA Modules:
  0.0 103.4 jit_solution(15761667683088226602)
XLA Ops:
  0.6 28.0 %exchange.1 = (f32[192,32768]{1,0:T(8,128)S(1)}, f32[192,32768]{1,0:T(8,128)S(1)}, f32[2,20,8,8192]{3,2,1,0:T(8,128)S(1)}, bf16[8,8,16384]{2,1,0:T(8,128)(2,1)S(1)}, f32[8,128]{1,0:T(8,128)}, /*index=5*/f32[8,128]{1,0:T(8,128)}) custom-call(bf16[1,192,65536]{2,1,0:T(8,128)(2,1)} %grads.1, f32[192,32768]{1,0:T(8,128)} %master.1, f32[192,32768]{1,0:T(8,128)} %one_in.3, ...), custom_call_target="tpu_custom_call" | custom-call | tf_op jit(solution)/shard_map/exchange/pallas_call | solution.py:445
  28.6 32.3 %moments.1 = (f32[192,32768]{1,0:T(8,128)S(1)}, f32[192,32768]{1,0:T(8,128)S(1)}, f32[2,20,8,8192]{3,2,1,0:T(8,128)S(1)}, bf16[8,8,16384]{2,1,0:T(8,128)(2,1)S(1...) custom-call(f32[192,32768]{1,0:T(8,128)S(1)} %get-tuple-element.19.m, ...), custom_call_target="tpu_custom_call", output_to_operand_aliasing={{0}: (0, {}), {1}: (1, {}), {2}: (2, {}), {3}: (3, {})} | custom-call | tf_op jit(solution)/shard_map/moments/pallas_call | solution.py:456
  61.0 25.6 %weights.1 = (bf16[24,8,32768]{2,1,0:T(8,128)(2,1)S(1)}, f32[8,128]{1,0:T(8,128)}) custom-call(f32[192,32768]{1,0:T(8,128)S(1)} %get-tuple-element.25.direction, f32[192,32768]{1,0:T(8,128)S(1)} %get-tuple-element.26.weight, f32[2,8,128]{2,1,0:T(8,128)} %get-tuple-element.27.stats), custom_call_target="tpu_custom_call" | custom-call | tf_op jit(solution)/shard_map/weights/pallas_call | solution.py:467
  86.5 16.8 %write.1 = (bf16[192,65536]{1,0:T(8,128)(2,1)}, f32[192,32768]{1,0:T(8,128)}) custom-call(f32[192,32768]{1,0:T(8,128)S(1)} %get-tuple-element.25.direction, f32[192,32768]{1,0:T(8,128)S(1)} %get-tuple-element.26.weight, bf16[24,8,32768]{2,1,0:T(8,128)(2,1)S(1)} %get-tuple-element.28.land, f32[8,128]{1,0:T(8,128)} %get-tuple-element.29.rate), custom_call_target="tpu_custom_call" | custom-call | tf_op jit(solution)/shard_map/write/pallas_call | solution.py:478

commit v5 on v4

--- a/solution.py
+++ b/solution.py
@@ -30,11 +30,11 @@
 LAND_SLOTS = 8
 STAGE_SLOTS = 9
 OWN_SLOTS = 6
-RING = 20
-LAG = 7
+RING = 10
+LAG = 4
 MOMENT_WIDTH = 2048
 MEAN_WIDTH = 2048
-CHUNK = 8192
+CHUNK = 16384
 SEND_SLOTS = 4
 WRITE_SLOTS = 5
 WRITE_CHUNK = 16384
@@ -237,8 +237,8 @@
         at = place(chunk)
         return (pltpu.make_async_copy(ring.at[0, slot], one_out.at[at], one_put.at[slot]), pltpu.make_async_copy(ring.at[1, slot], two_out.at[at], two_put.at[slot]))
 
-    def start(copies, priority=0):
-        for copy in copies:
+    def start(copies):
+        for priority, copy in enumerate(copies):
             copy.start(priority=priority)
 
     def wait(copies):
@@ -275,7 +275,7 @@
             return total + tree_sum([direction[:, at:at + LANES] * direction[:, at:at + LANES] for at in range(0, width, LANES)])
 
         total = lax.fori_loop(0, CHUNK // width, piece, jnp.zeros((GROUP, LANES), F32))
-        start(puts(chunk), priority=1)
+        start(puts(chunk))
         ahead = chunk + RING - LAG
 
         @pl.when(jnp.logical_and(ahead >= RING, ahead < chunks))
@@ -402,8 +402,8 @@
             return inner
 
         lax.fori_loop(0, WRITE_CHUNK // width, piece, 0, unroll=2)
-        for copy in puts(chunk):
-            copy.start()
+        for priority, copy in enumerate(puts(chunk)):
+            copy.start(priority=priority)
         return carry
 
     lax.fori_loop(0, chunks, one_chunk, 0)

time: 104 us -> 104 us (level)
  no operation moved by 1% of the time
where the time goes in v5:
time: 104 us
  Pallas kernels  103 us (99%)
    pallas_call x1, Pallas kernels, device_step(): pl.pallas_call(functools.partial(moment_kernel, groups, cols), out_shape=...  33 us
    pallas_call x1, Pallas kernels, device_step(): pl.pallas_call(functools.partial(exchange_kernel, sizes, groups, cols), o...  27.9 us
    pallas_call x1, Pallas kernels, device_step(): pl.pallas_call(functools.partial(weight_kernel, sizes, groups, cols), out...  25.4 us
    pallas_call x1, Pallas kernels, device_step(): pl.pallas_call(functools.partial(write_kernel, sizes, groups, cols), out_...  16.9 us

profile of v5, /device:TPU:0, one launch (start us, length us, event | category | flops | bytes accessed | tf_op | source)
XLA Modules:
  0.0 103.8 jit_solution(7116401898007314251)
XLA Ops:
  0.6 27.9 %exchange.1 = (f32[192,32768]{1,0:T(8,128)S(1)}, f32[192,32768]{1,0:T(8,128)S(1)}, f32[2,10,8,16384]{3,2,1,0:T(8,128)S(1)}, bf16[8,8,16384]{2,1,0:T(8,128)(2,1)S...) custom-call(bf16[1,192,65536]{2,1,0:T(8,128)(2,1)} %grads.1, f32[192,32768]{1,0:T(8,128)} %master.1, f32[192,32768]{1,0:T(8,128)} %one_in.3, ...), custom_call_target="tpu_custom_call" | custom-call | tf_op jit(solution)/shard_map/exchange/pallas_call | solution.py:445
  28.6 33.0 %moments.1 = (f32[192,32768]{1,0:T(8,128)S(1)}, f32[192,32768]{1,0:T(8,128)S(1)}, f32[2,10,8,16384]{3,2,1,0:T(8,128)S(1)}, bf16[8,8,16384]{2,1,0:T(8,128)(2,1)S(...) custom-call(f32[192,32768]{1,0:T(8,128)S(1)} %get-tuple-element.19.m, ...), custom_call_target="tpu_custom_call", output_to_operand_aliasing={{0}: (0, {}), {1}: (1, {}), {2}: (2, {}), {3}: (3, {})} | custom-call | tf_op jit(solution)/shard_map/moments/pallas_call | solution.py:456
  61.5 25.4 %weights.1 = (bf16[24,8,32768]{2,1,0:T(8,128)(2,1)S(1)}, f32[8,128]{1,0:T(8,128)}) custom-call(f32[192,32768]{1,0:T(8,128)S(1)} %get-tuple-element.25.direction, f32[192,32768]{1,0:T(8,128)S(1)} %get-tuple-element.26.weight, f32[2,8,128]{2,1,0:T(8,128)} %get-tuple-element.27.stats), custom_call_target="tpu_custom_call" | custom-call | tf_op jit(solution)/shard_map/weights/pallas_call | solution.py:467
  86.9 16.9 %write.1 = (bf16[192,65536]{1,0:T(8,128)(2,1)}, f32[192,32768]{1,0:T(8,128)}) custom-call(f32[192,32768]{1,0:T(8,128)S(1)} %get-tuple-element.25.direction, f32[192,32768]{1,0:T(8,128)S(1)} %get-tuple-element.26.weight, bf16[24,8,32768]{2,1,0:T(8,128)(2,1)S(1)} %get-tuple-element.28.land, f32[8,128]{1,0:T(8,128)} %get-tuple-element.29.rate), custom_call_target="tpu_custom_call" | custom-call | tf_op jit(solution)/shard_map/write/pallas_call | solution.py:478

commit v6 on v4

--- a/solution.py
+++ b/solution.py
@@ -31,8 +31,8 @@
 STAGE_SLOTS = 9
 OWN_SLOTS = 6
 RING = 20
-LAG = 7
-MOMENT_WIDTH = 2048
+LAG = 8
+MOMENT_WIDTH = 4096
 MEAN_WIDTH = 2048
 CHUNK = 8192
 SEND_SLOTS = 4
@@ -402,8 +402,8 @@
             return inner
 
         lax.fori_loop(0, WRITE_CHUNK // width, piece, 0, unroll=2)
-        for copy in puts(chunk):
-            copy.start()
+        for priority, copy in enumerate(puts(chunk)):
+            copy.start(priority=priority)
         return carry
 
     lax.fori_loop(0, chunks, one_chunk, 0)
@@ -432,7 +432,7 @@
         groups = blocks // GROUP
         kept = pltpu.VMEM((blocks, cols), F32)
         keep = functools.partial(pltpu.with_memory_space_constraint, memory_space=pltpu.VMEM)
-        tile = jax.ShapeDtypeStruct((GROUP, LANES), F32)
+        tile = pltpu.VMEM((GROUP, LANES), F32)
         state = jax.ShapeDtypeStruct((blocks, cols), F32)
 
         landed = pltpu.VMEM((groups, GROUP, cols), BF16)
@@ -455,14 +455,14 @@
 
         direction, weight, _, _, new_one, new_two, stats = pl.pallas_call(
             functools.partial(moment_kernel, groups, cols),
-            out_shape=(kept, kept, ring_shape, caught, state, state, jax.ShapeDtypeStruct((2, GROUP, LANES), F32)),
+            out_shape=(kept, kept, ring_shape, caught, state, state, pltpu.VMEM((2, GROUP, LANES), F32)),
             in_specs=[vmem] * 6 + [hbm] * 2,
             out_specs=[vmem, vmem, vmem, vmem, hbm, hbm, vmem],
             input_output_aliases={0: 0, 1: 1, 2: 2, 3: 3},
             scratch_shapes=[dma((RING,))] * 4,
             compiler_params=pltpu.CompilerParams(vmem_limit_bytes=SCOPE),
             name='moments',
-        )(mean, weight, ring, catch, clip, weight_stat, moment_one, moment_two)
+        )(mean, weight, ring, catch, keep(clip), keep(weight_stat), moment_one, moment_two)
 
         land, rate = pl.pallas_call(
             functools.partial(weight_kernel, sizes, groups, cols),
@@ -473,7 +473,7 @@
                             dma((SEND_SLOTS,)), dma((groups,)), dma((devices,)), dma((devices,))],
             compiler_params=pltpu.CompilerParams(collective_id=1, has_side_effects=True, vmem_limit_bytes=SCOPE),
             name='weights',
-        )(keep(direction), keep(weight), stats)
+        )(keep(direction), keep(weight), keep(stats))
 
         params, new_master = pl.pallas_call(
             functools.partial(write_kernel, sizes, groups, cols),
@@ -484,7 +484,7 @@
                             dma((WRITE_SLOTS,)), dma((groups,)), dma((WRITE_SLOTS,))],
             compiler_params=pltpu.CompilerParams(vmem_limit_bytes=SCOPE),
             name='write',
-        )(keep(direction), keep(weight), keep(land), rate)
+        )(keep(direction), keep(weight), keep(land), keep(rate))
         return params, new_master, new_one, new_two
 
     return jax.shard_map(device_step, mesh=mesh, in_specs=(P('data', None, 'model'), state_spec, state_spec, state_spec),

time: 104 us -> 109 us (1.048)
  local copies, waits for them, and re-layouts: 0 us -> 9.35 us
  Pallas kernels: 103 us -> 98.9 us
    unnamed x0 -> x4, local copies, waits for them, and re-layouts: none -> 9.35 us
    pallas_call x1, Pallas kernels: 25.6 us -> 24.3 us  [device_step(): pl.pallas_call(functools.partial(weight_kernel, sizes, groups, cols), out...]
    pallas_call x1, Pallas kernels: 32.3 us -> 31.1 us  [device_step(): pl.pallas_call(functools.partial(moment_kernel, groups, cols), out_shape=...]
where the time goes in v6:
time: 109 us
  Pallas kernels  98.9 us (91%)
  local copies, waits for them, and re-layouts  9.35 us (9%)
    pallas_call x1, Pallas kernels, device_step(): pl.pallas_call(functools.partial(moment_kernel, groups, cols), out_shape=...  31.1 us
    pallas_call x1, Pallas kernels, device_step(): pl.pallas_call(functools.partial(exchange_kernel, sizes, groups, cols), o...  27.4 us
    pallas_call x1, Pallas kernels, device_step(): pl.pallas_call(functools.partial(weight_kernel, sizes, groups, cols), out...  24.3 us
    pallas_call x1, Pallas kernels, device_step(): pl.pallas_call(functools.partial(write_kernel, sizes, groups, cols), out_...  16.2 us
    unnamed x4, local copies, waits for them, and re-layouts  9.35 us

profile of v6, /device:TPU:0, one launch (start us, length us, event | category | flops | bytes accessed | tf_op | source)
XLA Modules:
  0.0 109.0 jit_solution(7391524375888558232)
XLA Ops:
  0.6 27.4 %exchange.1 = (f32[192,32768]{1,0:T(8,128)S(1)}, f32[192,32768]{1,0:T(8,128)S(1)}, f32[2,20,8,8192]{3,2,1,0:T(8,128)S(1)}, bf16[8,8,16384]{2,1,0:T(8,128)(2,1)S(...) custom-call(bf16[1,192,65536]{2,1,0:T(8,128)(2,1)} %grads.1, f32[192,32768]{1,0:T(8,128)} %master.1, f32[192,32768]{1,0:T(8,128)} %one_in.3, ...), custom_call_target="tpu_custom_call" | custom-call | tf_op jit(solution)/shard_map/exchange/pallas_call | solution.py:445
  28.0 31.1 %moments.1 = (f32[192,32768]{1,0:T(8,128)S(1)}, f32[192,32768]{1,0:T(8,128)S(1)}, f32[2,20,8,8192]{3,2,1,0:T(8,128)S(1)}, bf16[8,8,16384]{2,1,0:T(8,128)(2,1)S(1...) custom-call(f32[192,32768]{1,0:T(8,128)S(1)} %get-tuple-element.19.m, ...), custom_call_target="tpu_custom_call", output_to_operand_aliasing={{0}: (0, {}), {1}: (1, {}), {2}: (2, {}), {3}: (3, {})} | custom-call | tf_op jit(solution)/shard_map/moments/pallas_call | solution.py:456
  59.1 24.3 %weights.1 = (bf16[24,8,32768]{2,1,0:T(8,128)(2,1)S(1)}, f32[8,128]{1,0:T(8,128)S(1)}) custom-call(f32[192,32768]{1,0:T(8,128)S(1)} %get-tuple-element.25.direction, f32[192,32768]{1,0:T(8,128)S(1)} %get-tuple-element.26.weight, f32[2,8,128]{2,1,0:T(8,128)S(1)} %get-tuple-element.27.stats), custom_call_target="tpu_custom_call" | custom-call | tf_op jit(solution)/shard_map/weights/pallas_call | solution.py:467
  83.4 0.0 copy-start
  83.4 4.8 %copy-done = bf16[24,8,32768]{2,1,0:T(8,128)(2,1)} copy-done((bf16[24,8,32768]{2,1,0:T(8,128)(2,1)}, bf16[24,8,32768]{2,1,0:T(8,128)(2,1)S(1)}, u32[]{:S(2)}) %copy-start) | copy-done | bytes 12582936
  88.2 0.0 copy-start.1
  88.2 4.6 %copy-done.1 = bf16[24,8,32768]{2,1,0:T(8,128)(2,1)S(1)} copy-done((bf16[24,8,32768]{2,1,0:T(8,128)(2,1)S(1)}, bf16[24,8,32768]{2,1,0:T(8,128)(2,1)}, u32[]{:S(2)}) %copy-start.1) | copy-done | bytes 12582936
  92.8 16.2 %write.1 = (bf16[192,65536]{1,0:T(8,128)(2,1)}, f32[192,32768]{1,0:T(8,128)}) custom-call(f32[192,32768]{1,0:T(8,128)S(1)} %get-tuple-element.25.direction, f32[192,32768]{1,0:T(8,128)S(1)} %get-tuple-element.26.weight, bf16[24,8,32768]{2,1,0:T(8,128)(2,1)S(1)} %copy-done.1, f32[8,128]{1,0:T(8,128)S(1)} %get-tuple-element.29.rate), custom_call_target="tpu_custom_call" | custom-call | tf_op jit(solution)/shard_map/write/pallas_call | solution.py:478
Async XLA Ops:
  83.4 4.8 %copy-start = (bf16[24,8,32768]{2,1,0:T(8,128)(2,1)}, bf16[24,8,32768]{2,1,0:T(8,128)(2,1)S(1)}, u32[]{:S(2)}) copy-start(bf16[24,8,32768]{2,1,0:T(8,128)(2,1)S(1)} %get-tuple-element.28.land) | copy-start | bytes 37748740
  88.2 4.6 %copy-start.1 = (bf16[24,8,32768]{2,1,0:T(8,128)(2,1)S(1)}, bf16[24,8,32768]{2,1,0:T(8,128)(2,1)}, u32[]{:S(2)}) copy-start(bf16[24,8,32768]{2,1,0:T(8,128)(2,1)} %copy-done) | copy-start | bytes 37748740

commit v7 on v6

--- a/solution.py
+++ b/solution.py
@@ -36,6 +36,8 @@
 MEAN_WIDTH = 2048
 CHUNK = 8192
 SEND_SLOTS = 4
+RIDE = 12
+RIDE_SLOTS = 2
 WRITE_SLOTS = 5
 WRITE_CHUNK = 16384
 
@@ -309,18 +311,19 @@
     return out
 
 
-def weight_kernel(sizes, groups, cols, direction, weight, stats, land, rate, slots, packed, send_sem, recv_sem, small_send, small_recv):
+def weight_kernel(sizes, groups, cols, direction, weight, stats, land, rate, ride, slots, packed, spare, send_sem, recv_sem, ride_sem, small_send, small_recv):
     model_size, data_size = sizes
     data = lax.axis_index('data')
     me, others = peers(model_size, data_size)
     peer_device = (lax.axis_index('model'), lax.rem(data + 1, data_size))
+    sent = groups - RIDE
     enter(others)
     slots[me] = stats[...]
     share(me, others, stats, slots, small_send, small_recv)
     lane_ids = lanes_of()
     dir_sq = segment_sums(tree_sum([slots[index, 0] for index in range(model_size * data_size)]))
     weight_sq = segment_sums(tree_sum([slots[index, 1] for index in range(model_size * data_size)]))
-    rate[...] = LEARN_RATE * (jnp.sqrt(weight_sq) / jnp.sqrt(dir_sq))
+    rate[0] = LEARN_RATE * (jnp.sqrt(weight_sq) / jnp.sqrt(dir_sq))
     width = 1024
 
     def send_copy(group):
@@ -328,6 +331,20 @@
         return pltpu.make_async_remote_copy(src_ref=packed.at[slot], dst_ref=land.at[group], send_sem=send_sem.at[slot], recv_sem=recv_sem.at[group],
                                             device_id=peer_device, device_id_type=MESH)
 
+    def ride_copy(index):
+        slot = lax.rem(index, RIDE_SLOTS)
+        return pltpu.make_async_copy(spare.at[slot], ride.at[index], ride_sem.at[slot])
+
+    def pack(group, target, slot):
+        group_rate = jnp.sum(jnp.where(lane_ids == group, rate[0], 0.0), axis=1, keepdims=True)
+
+        def piece(index, inner):
+            at = pl.ds(pl.multiple_of(index * width, width), width)
+            target[slot, :, at] = (weight[rows(group), at] - group_rate * direction[rows(group), at]).astype(BF16)
+            return inner
+
+        lax.fori_loop(0, cols // width, piece, 0, unroll=2)
+
     def one_group(group, carry):
         slot = lax.rem(group, SEND_SLOTS)
 
@@ -335,26 +352,31 @@
         def _():
             send_copy(group - SEND_SLOTS).wait_send()
 
-        group_rate = jnp.sum(jnp.where(lane_ids == group, rate[...], 0.0), axis=1, keepdims=True)
-
-        def piece(index, inner):
-            at = pl.ds(pl.multiple_of(index * width, width), width)
-            packed[slot, :, at] = (weight[rows(group), at] - group_rate * direction[rows(group), at]).astype(BF16)
-            return inner
-
-        lax.fori_loop(0, cols // width, piece, 0, unroll=2)
+        pack(group, packed, slot)
         send_copy(group).start()
-        return carry
-
-    lax.fori_loop(0, groups, one_group, 0)
+
+        @pl.when(group < RIDE)
+        def _():
+            @pl.when(group >= RIDE_SLOTS)
+            def _():
+                ride_copy(group - RIDE_SLOTS).wait()
+
+            pack(sent + group, spare, lax.rem(group, RIDE_SLOTS))
+            ride_copy(group).start()
+
+        return carry
+
+    lax.fori_loop(0, sent, one_group, 0)
 
     def finish(group, carry):
         send_copy(group).wait_recv()
         return carry
 
-    lax.fori_loop(0, groups, finish, 0)
-    for group in range(groups - SEND_SLOTS, groups):
+    lax.fori_loop(0, sent, finish, 0)
+    for group in range(sent - SEND_SLOTS, sent):
         send_copy(group).wait_send()
+    for index in range(RIDE - RIDE_SLOTS, RIDE):
+        ride_copy(index).wait()
 
 
 def write_kernel(sizes, groups, cols, direction, weight, land, rate, params, master, fresh, packed, master_sem, land_sem, own_sem):
@@ -382,7 +404,7 @@
         slot = lax.rem(chunk, WRITE_SLOTS)
         group = chunk // per_group
 
-        @pl.when(lax.rem(chunk, per_group) == 0)
+        @pl.when(jnp.logical_and(lax.rem(chunk, per_group) == 0, group < groups - RIDE))
         def _():
             land_copy(group).start()
 
@@ -391,7 +413,7 @@
             for copy in puts(chunk - WRITE_SLOTS):
                 copy.wait()
 
-        group_rate = jnp.sum(jnp.where(lane_ids == group, rate[...], 0.0), axis=1, keepdims=True)
+        group_rate = jnp.sum(jnp.where(lane_ids == group, rate[0], 0.0), axis=1, keepdims=True)
 
         def piece(index, inner):
             near = pl.ds(pl.multiple_of(index * width, width), width)
@@ -412,10 +434,29 @@
         land_copy(group).wait()
         return carry
 
-    lax.fori_loop(0, groups, finish, 0)
+    lax.fori_loop(0, groups - RIDE, finish, 0)
     for chunk in range(chunks - WRITE_SLOTS, chunks):
         for copy in puts(chunk):
             copy.wait()
+
+
+def place_kernel(sizes, groups, cols, given, params_in, params, put_sem):
+    data_size = sizes[1]
+    peer = lax.rem(lax.axis_index('data') + 1, data_size)
+
+    def put(index):
+        return pltpu.make_async_copy(given.at[index], params.at[rows(groups - RIDE + index), pl.ds(pl.multiple_of(peer * cols, LANES), cols)], put_sem.at[index])
+
+    def begin(index, carry):
+        put(index).start()
+        return carry
+
+    def finish(index, carry):
+        put(index).wait()
+        return carry
+
+    lax.fori_loop(0, RIDE, begin, 0)
+    lax.fori_loop(0, RIDE, finish, 0)
 
 
 def solution(mesh):
@@ -435,9 +476,11 @@
         tile = pltpu.VMEM((GROUP, LANES), F32)
         state = jax.ShapeDtypeStruct((blocks, cols), F32)
 
-        landed = pltpu.VMEM((groups, GROUP, cols), BF16)
+        landed = pltpu.VMEM((groups - RIDE, GROUP, cols), BF16)
+        riding = jax.ShapeDtypeStruct((RIDE, GROUP, cols), BF16)
         ring_shape = pltpu.VMEM((2, RING, GROUP, CHUNK), F32)
-        landed = pltpu.VMEM((groups, GROUP, cols), BF16)
+        landed = pltpu.VMEM((groups - RIDE, GROUP, cols), BF16)
+        riding = jax.ShapeDtypeStruct((RIDE, GROUP, cols), BF16)
         parts = groups * (cols // PART)
 
         caught = pltpu.VMEM((LAND_SLOTS, GROUP, PART), BF16)
@@ -464,16 +507,19 @@
             name='moments',
         )(mean, weight, ring, catch, keep(clip), keep(weight_stat), moment_one, moment_two)
 
-        land, rate = pl.pallas_call(
+        land, rate, ride = pl.pallas_call(
             functools.partial(weight_kernel, sizes, groups, cols),
-            out_shape=(landed, tile),
+            out_shape=(landed, pltpu.VMEM((2, GROUP, LANES), F32), riding),
             in_specs=[vmem] * 3,
-            out_specs=[vmem] * 2,
-            scratch_shapes=[pltpu.VMEM((devices, 2, GROUP, LANES), F32), pltpu.VMEM((SEND_SLOTS, GROUP, cols), BF16),
-                            dma((SEND_SLOTS,)), dma((groups,)), dma((devices,)), dma((devices,))],
+            out_specs=[vmem, vmem, hbm],
+            input_output_aliases={2: 1},
+            scratch_shapes=[pltpu.VMEM((devices, 2, GROUP, LANES), F32), pltpu.VMEM((SEND_SLOTS, GROUP, cols), BF16), pltpu.VMEM((RIDE_SLOTS, GROUP, cols), BF16),
+                            dma((SEND_SLOTS,)), dma((groups - RIDE,)), dma((RIDE_SLOTS,)), dma((devices,)), dma((devices,))],
             compiler_params=pltpu.CompilerParams(collective_id=1, has_side_effects=True, vmem_limit_bytes=SCOPE),
             name='weights',
         )(keep(direction), keep(weight), keep(stats))
+
+        given = lax.ppermute(ride, 'data', [(rank, (rank + 1) % sizes[1]) for rank in range(sizes[1])])
 
         params, new_master = pl.pallas_call(
             functools.partial(write_kernel, sizes, groups, cols),
@@ -485,6 +531,16 @@
             compiler_params=pltpu.CompilerParams(vmem_limit_bytes=SCOPE),
             name='write',
         )(keep(direction), keep(weight), keep(land), keep(rate))
+        params = pl.pallas_call(
+            functools.partial(place_kernel, sizes, groups, cols),
+            out_shape=jax.ShapeDtypeStruct((blocks, sizes[1] * cols), BF16),
+            in_specs=[vmem, hbm],
+            out_specs=hbm,
+            input_output_aliases={1: 0},
+            scratch_shapes=[dma((RIDE,))],
+            compiler_params=pltpu.CompilerParams(vmem_limit_bytes=SCOPE),
+            name='place',
+        )(keep(given), params)
         return params, new_master, new_one, new_two
 
     return jax.shard_map(device_step, mesh=mesh, in_specs=(P('data', None, 'model'), state_spec, state_spec, state_spec),

time: 109 us -> 91.8 us (0.84)
  local copies, waits for them, and re-layouts: 9.35 us -> 0 us
  Pallas kernels: 98.9 us -> 90.6 us
    unnamed x4 -> x0, local copies, waits for them, and re-layouts: 9.35 us -> none
    pallas_call x1, Pallas kernels: 24.3 us -> 15.2 us  [device_step(): pl.pallas_call(functools.partial(weight_kernel, sizes, groups, cols), out...]
    pallas_call x0 -> x1, Pallas kernels: none -> 2.76 us  [device_step(): pl.pallas_call(functools.partial(place_kernel, sizes, groups, cols), out_...]
    pallas_call x1, Pallas kernels: 16.2 us -> 14.3 us  [device_step(): pl.pallas_call(functools.partial(write_kernel, sizes, groups, cols), out_...]
  transfers between devices with their start and end apart: 0 -> 1, of which waited for: 0 -> 0; matrix products, arithmetic and copies ran while one was open for 0% -> 0% of each run, Pallas kernels for 0% -> 16%
where the time goes in v7:
time: 91.8 us; the launch traced here: 91.7 us
  Pallas kernels  90.6 us (99%)
    pallas_call x1, Pallas kernels, device_step(): pl.pallas_call(functools.partial(moment_kernel, groups, cols), out_shape=...  31 us
    pallas_call x1, Pallas kernels, device_step(): pl.pallas_call(functools.partial(exchange_kernel, sizes, groups, cols), o...  27.4 us
    pallas_call x1, Pallas kernels, device_step(): pl.pallas_call(functools.partial(weight_kernel, sizes, groups, cols), out...  15.2 us
    pallas_call x1, Pallas kernels, device_step(): pl.pallas_call(functools.partial(write_kernel, sizes, groups, cols), out_...  14.3 us
    pallas_call x1, Pallas kernels, device_step(): pl.pallas_call(functools.partial(place_kernel, sizes, groups, cols), out_...  2.76 us
  transfers between devices with their start and end apart: 1, of which 0 were waited for; matrix products, arithmetic and copies ran while one was open for 0% of the time, Pallas kernels for 16%

profile of v7, /device:TPU:0, one launch (start us, length us, event | category | flops | bytes accessed | tf_op | source)
XLA Modules:
  0.0 91.7 jit_solution(17294898545543699496)
XLA Ops:
  0.6 27.4 %exchange.1 = (f32[192,32768]{1,0:T(8,128)S(1)}, f32[192,32768]{1,0:T(8,128)S(1)}, f32[2,20,8,8192]{3,2,1,0:T(8,128)S(1)}, bf16[8,8,16384]{2,1,0:T(8,128)(2,1)S(...) custom-call(bf16[1,192,65536]{2,1,0:T(8,128)(2,1)} %grads.1, f32[192,32768]{1,0:T(8,128)} %master.1, f32[192,32768]{1,0:T(8,128)} %one_in.3, ...), custom_call_target="tpu_custom_call" | custom-call | tf_op jit(solution)/shard_map/exchange/pallas_call | solution.py:488
  28.0 31.0 %moments.1 = (f32[192,32768]{1,0:T(8,128)S(1)}, f32[192,32768]{1,0:T(8,128)S(1)}, f32[2,20,8,8192]{3,2,1,0:T(8,128)S(1)}, bf16[8,8,16384]{2,1,0:T(8,128)(2,1)S(1...) custom-call(f32[192,32768]{1,0:T(8,128)S(1)} %get-tuple-element.20.m, ...), custom_call_target="tpu_custom_call", output_to_operand_aliasing={{0}: (0, {}), {1}: (1, {}), {2}: (2, {}), {3}: (3, {})} | custom-call | tf_op jit(solution)/shard_map/moments/pallas_call | solution.py:499
  59.0 15.2 %weights.1 = (bf16[12,8,32768]{2,1,0:T(8,128)(2,1)S(1)}, f32[2,8,128]{2,1,0:T(8,128)S(1)}, bf16[12,8,32768]{2,1,0:T(8,128)(2,1)}) custom-call(f32[192,32768]{1,0:T(8,128)S(1)} %get-tuple-element.26.direction, f32[192,32768]{1,0:T(8,128)S(1)} %get-tuple-element.27.weight, f32[2,8,128]{2,1,0:T(8,128)S(1)} %get-tuple-element.28.stats), custom_call_target="tpu_custom_call", output_to_operand_aliasing={{1}: (2, {})} | custom-call | tf_op jit(solution)/shard_map/weights/pallas_call | solution.py:510
  74.2 0.4 collective-permute-start
  74.6 14.3 %write.1 = (bf16[192,65536]{1,0:T(8,128)(2,1)}, f32[192,32768]{1,0:T(8,128)}) custom-call(f32[192,32768]{1,0:T(8,128)S(1)} %get-tuple-element.26.direction, f32[192,32768]{1,0:T(8,128)S(1)} %get-tuple-element.27.weight, bf16[12,8,32768]{2,1,0:T(8,128)(2,1)S(1)} %get-tuple-element.30.land, f32[2,8,128]{2,1,0:T(8,128)S(1)} %get-tuple-element.31.rate), custom_call_target="tpu_custom_call" | custom-call | tf_op jit(solution)/shard_map/write/pallas_call | solution.py:524
  88.9 0.0 collective-permute-done.given
  89.0 2.8 %place.1 = bf16[192,65536]{1,0:T(8,128)(2,1)} custom-call(bf16[12,8,32768]{2,1,0:T(8,128)(2,1)S(1)} %collective-permute-done.given, bf16[192,65536]{1,0:T(8,128)(2,1)} %get-tuple-element.32.params_in), custom_call_target="tpu_custom_call", output_to_operand_aliasing={{}: (1, {})} | custom-call | tf_op jit(solution)/shard_map/place/pallas_call | solution.py:534
Async XLA Ops:
  74.2 14.7 %collective-permute-start = (bf16[12,8,32768]{2,1,0:T(8,128)(2,1)}, bf16[12,8,32768]{2,1,0:T(8,128)(2,1)S(1)}, u32[]{:S(2)}, u32[]{:S(2)}) collective-permute-start(bf16[12,8,32768]{2,1,0:T(8,128)(2,1)} %get-tuple-element.29), channel_id=1, source_target_pairs={{0,1},{1,0},{2,3},{3,2},{4,5},{5,4},{6,7},{7,6}} | collective-permute-start | bytes 18874376 | tf_op jit(solution)/shard_map/ppermute | solution.py:522

commit v8 on v7

--- a/solution.py
+++ b/solution.py
@@ -25,18 +25,18 @@
 LANES = 128
 GROUP = 8
 
-PART = 16384
-AHEAD = 4
-LAND_SLOTS = 8
-STAGE_SLOTS = 9
-OWN_SLOTS = 6
+PART = 32768
+AHEAD = 2
+LAND_SLOTS = 4
+STAGE_SLOTS = 4
+OWN_SLOTS = 3
 RING = 20
 LAG = 8
 MOMENT_WIDTH = 4096
 MEAN_WIDTH = 2048
 CHUNK = 8192
 SEND_SLOTS = 4
-RIDE = 12
+RIDE = 16
 RIDE_SLOTS = 2
 WRITE_SLOTS = 5
 WRITE_CHUNK = 16384
@@ -145,7 +145,7 @@
     lane_ids = lanes_of()
     width = MEAN_WIDTH
     zero = jnp.zeros((GROUP, LANES), F32)
-    first_ring = parts - RING // 2
+    first_ring = parts - RING // 4
 
     def one_part(index, carry):
         total, stat = carry
@@ -195,8 +195,8 @@
 
         @pl.when(index >= first_ring)
         def _():
-            for late in range(2):
-                for copy in ring_copies((index - first_ring) * 2 + late):
+            for late in range(4):
+                for copy in ring_copies((index - first_ring) * 4 + late):
                     copy.start()
 
         return total + grad_sum, put_lane(stat, lane_ids, index // per_group, weight_sum)
@@ -355,15 +355,16 @@
         pack(group, packed, slot)
         send_copy(group).start()
 
-        @pl.when(group < RIDE)
-        def _():
-            @pl.when(group >= RIDE_SLOTS)
+        def one_ride(index, inner):
+            @pl.when(index >= RIDE_SLOTS)
             def _():
-                ride_copy(group - RIDE_SLOTS).wait()
-
-            pack(sent + group, spare, lax.rem(group, RIDE_SLOTS))
-            ride_copy(group).start()
-
+                ride_copy(index - RIDE_SLOTS).wait()
+
+            pack(sent + index, spare, lax.rem(index, RIDE_SLOTS))
+            ride_copy(index).start()
+            return inner
+
+        lax.fori_loop(group * RIDE // sent, (group + 1) * RIDE // sent, one_ride, 0)
         return carry
 
     lax.fori_loop(0, sent, one_group, 0)

time: 91.8 us -> 98.1 us (1.069)
  Pallas kernels: 90.6 us -> 96.8 us
    pallas_call x1, Pallas kernels: 27.4 us -> 34 us  [device_step(): pl.pallas_call(functools.partial(exchange_kernel, sizes, groups, cols), o...]
  transfers between devices with their start and end apart: 1 -> 1, of which waited for: 0 -> 0; matrix products, arithmetic and copies ran while one was open for 0% -> 0% of each run, Pallas kernels for 16% -> 14%
where the time goes in v8:
time: 98.1 us; the launch traced here: 97.8 us
  Pallas kernels  96.8 us (99%)
    pallas_call x1, Pallas kernels, device_step(): pl.pallas_call(functools.partial(exchange_kernel, sizes, groups, cols), o...  34 us
    pallas_call x1, Pallas kernels, device_step(): pl.pallas_call(functools.partial(moment_kernel, groups, cols), out_shape=...  31 us
    pallas_call x1, Pallas kernels, device_step(): pl.pallas_call(functools.partial(weight_kernel, sizes, groups, cols), out...  14.5 us
    pallas_call x1, Pallas kernels, device_step(): pl.pallas_call(functools.partial(write_kernel, sizes, groups, cols), out_...  13.8 us
    pallas_call x1, Pallas kernels, device_step(): pl.pallas_call(functools.partial(place_kernel, sizes, groups, cols), out_...  3.43 us
  transfers between devices with their start and end apart: 1, of which 0 were waited for; matrix products, arithmetic and copies ran while one was open for 0% of the time, Pallas kernels for 14%

profile of v8, /device:TPU:0, one launch (start us, length us, event | category | flops | bytes accessed | tf_op | source)
XLA Modules:
  0.0 97.8 jit_solution(3226572222423145693)
XLA Ops:
  0.6 34.0 %exchange.1 = (f32[192,32768]{1,0:T(8,128)S(1)}, f32[192,32768]{1,0:T(8,128)S(1)}, f32[2,20,8,8192]{3,2,1,0:T(8,128)S(1)}, bf16[4,8,32768]{2,1,0:T(8,128)(2,1)S(...) custom-call(bf16[1,192,65536]{2,1,0:T(8,128)(2,1)} %grads.1, f32[192,32768]{1,0:T(8,128)} %master.1, f32[192,32768]{1,0:T(8,128)} %one_in.3, ...), custom_call_target="tpu_custom_call" | custom-call | tf_op jit(solution)/shard_map/exchange/pallas_call | solution.py:489
  34.7 31.0 %moments.1 = (f32[192,32768]{1,0:T(8,128)S(1)}, f32[192,32768]{1,0:T(8,128)S(1)}, f32[2,20,8,8192]{3,2,1,0:T(8,128)S(1)}, bf16[4,8,32768]{2,1,0:T(8,128)(2,1)S(1...) custom-call(f32[192,32768]{1,0:T(8,128)S(1)} %get-tuple-element.20.m, ...), custom_call_target="tpu_custom_call", output_to_operand_aliasing={{0}: (0, {}), {1}: (1, {}), {2}: (2, {}), {3}: (3, {})} | custom-call | tf_op jit(solution)/shard_map/moments/pallas_call | solution.py:500
  65.7 14.5 %weights.1 = (bf16[8,8,32768]{2,1,0:T(8,128)(2,1)S(1)}, f32[2,8,128]{2,1,0:T(8,128)S(1)}, bf16[16,8,32768]{2,1,0:T(8,128)(2,1)}) custom-call(f32[192,32768]{1,0:T(8,128)S(1)} %get-tuple-element.26.direction, f32[192,32768]{1,0:T(8,128)S(1)} %get-tuple-element.27.weight, f32[2,8,128]{2,1,0:T(8,128)S(1)} %get-tuple-element.28.stats), custom_call_target="tpu_custom_call", output_to_operand_aliasing={{1}: (2, {})} | custom-call | tf_op jit(solution)/shard_map/weights/pallas_call | solution.py:511
  80.2 0.3 collective-permute-start
  80.5 13.8 %write.1 = (bf16[192,65536]{1,0:T(8,128)(2,1)}, f32[192,32768]{1,0:T(8,128)}) custom-call(f32[192,32768]{1,0:T(8,128)S(1)} %get-tuple-element.26.direction, f32[192,32768]{1,0:T(8,128)S(1)} %get-tuple-element.27.weight, bf16[8,8,32768]{2,1,0:T(8,128)(2,1)S(1)} %get-tuple-element.30.land, f32[2,8,128]{2,1,0:T(8,128)S(1)} %get-tuple-element.31.rate), custom_call_target="tpu_custom_call" | custom-call | tf_op jit(solution)/shard_map/write/pallas_call | solution.py:525
  94.3 0.0 collective-permute-done.given
  94.3 3.4 %place.1 = bf16[192,65536]{1,0:T(8,128)(2,1)} custom-call(bf16[16,8,32768]{2,1,0:T(8,128)(2,1)S(1)} %collective-permute-done.given, bf16[192,65536]{1,0:T(8,128)(2,1)} %get-tuple-element.32.params_in), custom_call_target="tpu_custom_call", output_to_operand_aliasing={{}: (1, {})} | custom-call | tf_op jit(solution)/shard_map/place/pallas_call | solution.py:535
Async XLA Ops:
  80.2 14.2 %collective-permute-start = (bf16[16,8,32768]{2,1,0:T(8,128)(2,1)}, bf16[16,8,32768]{2,1,0:T(8,128)(2,1)S(1)}, u32[]{:S(2)}, u32[]{:S(2)}) collective-permute-start(bf16[16,8,32768]{2,1,0:T(8,128)(2,1)} %get-tuple-element.29), channel_id=1, source_target_pairs={{0,1},{1,0},{2,3},{3,2},{4,5},{5,4},{6,7},{7,6}} | collective-permute-start | bytes 25165832 | tf_op jit(solution)/shard_map/ppermute | solution.py:523

commit v9 on v8

--- a/solution.py
+++ b/solution.py
@@ -25,19 +25,19 @@
 LANES = 128
 GROUP = 8
 
-PART = 32768
-AHEAD = 2
-LAND_SLOTS = 4
-STAGE_SLOTS = 4
-OWN_SLOTS = 3
-RING = 20
-LAG = 8
+PART = 16384
+AHEAD = 4
+LAND_SLOTS = 8
+STAGE_SLOTS = 12
+OWN_SLOTS = 7
+RING = 18
+LAG = 7
 MOMENT_WIDTH = 4096
 MEAN_WIDTH = 2048
 CHUNK = 8192
-SEND_SLOTS = 4
-RIDE = 16
-RIDE_SLOTS = 2
+SEND_SLOTS = 3
+RIDE = 17
+RIDE_SLOTS = 4
 WRITE_SLOTS = 5
 WRITE_CHUNK = 16384
 
@@ -90,7 +90,7 @@
         copy.wait_send()
 
 
-def exchange_kernel(sizes, groups, cols, grads, master, one_in, two_in, mean_ref, weight_ref, ring, land, clip_ref, stat_ref, stage, own, part, slots,
+def exchange_kernel(sizes, groups, cols, grads, master, one_in, two_in, mean_ref, weight_ref, ring, stage, clip_ref, stat_ref, land, own, part, slots,
                     stage_sem, send_sem, recv_sem, free_sem, own_sem, weight_sem, ring_sem, small_send, small_recv):
     model_size, data_size = sizes
     data = lax.axis_index('data')
@@ -145,7 +145,7 @@
     lane_ids = lanes_of()
     width = MEAN_WIDTH
     zero = jnp.zeros((GROUP, LANES), F32)
-    first_ring = parts - RING // 4
+    first_ring = parts - RING // 2
 
     def one_part(index, carry):
         total, stat = carry
@@ -195,8 +195,8 @@
 
         @pl.when(index >= first_ring)
         def _():
-            for late in range(4):
-                for copy in ring_copies((index - first_ring) * 4 + late):
+            for late in range(2):
+                for copy in ring_copies((index - first_ring) * 2 + late):
                     copy.start()
 
         return total + grad_sum, put_lane(stat, lane_ids, index // per_group, weight_sum)
@@ -219,7 +219,7 @@
     lax.fori_loop(0, RING, finish, 0)
 
 
-def moment_kernel(groups, cols, mean_in, weight_in, ring_in, land_in, clip, weight_stat, one_in, two_in, dir_ref, weight_ref, ring, land, one_out, two_out, stat_ref,
+def moment_kernel(groups, cols, mean_in, weight_in, ring_in, stage_in, clip, weight_stat, one_in, two_in, dir_ref, weight_ref, ring, stage, one_out, two_out, stat_ref,
                   one_get, two_get, one_put, two_put):
     per_group = cols // CHUNK
     chunks = groups * per_group
@@ -484,14 +484,14 @@
         riding = jax.ShapeDtypeStruct((RIDE, GROUP, cols), BF16)
         parts = groups * (cols // PART)
 
-        caught = pltpu.VMEM((LAND_SLOTS, GROUP, PART), BF16)
-
-        mean, weight, ring, catch, clip, weight_stat = pl.pallas_call(
+        staged = pltpu.VMEM((STAGE_SLOTS, GROUP, PART), BF16)
+
+        mean, weight, ring, stage, clip, weight_stat = pl.pallas_call(
             functools.partial(exchange_kernel, sizes, groups, cols),
-            out_shape=(kept, kept, ring_shape, caught, tile, tile),
+            out_shape=(kept, kept, ring_shape, staged, tile, tile),
             in_specs=[hbm] * 4,
             out_specs=[vmem] * 6,
-            scratch_shapes=[pltpu.VMEM((STAGE_SLOTS, GROUP, PART), BF16), pltpu.VMEM((OWN_SLOTS, GROUP, PART), BF16), pltpu.VMEM((GROUP, LANES), F32), pltpu.VMEM((devices, GROUP, LANES), F32),
+            scratch_shapes=[pltpu.VMEM((LAND_SLOTS, GROUP, PART), BF16), pltpu.VMEM((OWN_SLOTS, GROUP, PART), BF16), pltpu.VMEM((GROUP, LANES), F32), pltpu.VMEM((devices, GROUP, LANES), F32),
                             dma((STAGE_SLOTS,)), dma((STAGE_SLOTS,)), dma((LAND_SLOTS,)), pltpu.SemaphoreType.REGULAR, dma((OWN_SLOTS,)), dma((parts,)), dma((2, RING)), dma((devices,)), dma((devices,))],
             compiler_params=pltpu.CompilerParams(collective_id=0, has_side_effects=True, vmem_limit_bytes=SCOPE),
             name='exchange',
@@ -499,14 +499,14 @@
 
         direction, weight, _, _, new_one, new_two, stats = pl.pallas_call(
             functools.partial(moment_kernel, groups, cols),
-            out_shape=(kept, kept, ring_shape, caught, state, state, pltpu.VMEM((2, GROUP, LANES), F32)),
+            out_shape=(kept, kept, ring_shape, staged, state, state, pltpu.VMEM((2, GROUP, LANES), F32)),
             in_specs=[vmem] * 6 + [hbm] * 2,
             out_specs=[vmem, vmem, vmem, vmem, hbm, hbm, vmem],
             input_output_aliases={0: 0, 1: 1, 2: 2, 3: 3},
             scratch_shapes=[dma((RING,))] * 4,
             compiler_params=pltpu.CompilerParams(vmem_limit_bytes=SCOPE),
             name='moments',
-        )(mean, weight, ring, catch, keep(clip), keep(weight_stat), moment_one, moment_two)
+        )(mean, weight, ring, stage, keep(clip), keep(weight_stat), moment_one, moment_two)
 
         land, rate, ride = pl.pallas_call(
             functools.partial(weight_kernel, sizes, groups, cols),

time: 98.1 us -> 90.7 us (0.925)
  Pallas kernels: 96.8 us -> 89.7 us
    pallas_call x1, Pallas kernels: 34 us -> 27.5 us  [device_step(): pl.pallas_call(functools.partial(exchange_kernel, sizes, groups, cols), o...]
  transfers between devices with their start and end apart: 1 -> 1, of which waited for: 0 -> 1; matrix products, arithmetic and copies ran while one was open for 0% -> 0% of each run, Pallas kernels for 14% -> 15%
where the time goes in v9:
time: 90.7 us; the launch traced here: 90.6 us
  Pallas kernels  89.7 us (99%)
    pallas_call x1, Pallas kernels, device_step(): pl.pallas_call(functools.partial(moment_kernel, groups, cols), out_shape=...  31.2 us
    pallas_call x1, Pallas kernels, device_step(): pl.pallas_call(functools.partial(exchange_kernel, sizes, groups, cols), o...  27.5 us
    pallas_call x1, Pallas kernels, device_step(): pl.pallas_call(functools.partial(weight_kernel, sizes, groups, cols), out...  13.8 us
    pallas_call x1, Pallas kernels, device_step(): pl.pallas_call(functools.partial(write_kernel, sizes, groups, cols), out_...  13.7 us
    pallas_call x1, Pallas kernels, device_step(): pl.pallas_call(functools.partial(place_kernel, sizes, groups, cols), out_...  3.58 us
  transfers between devices with their start and end apart: 1, of which 1 were waited for; matrix products, arithmetic and copies ran while one was open for 0% of the time, Pallas kernels for 15%

profile of v9, /device:TPU:0, one launch (start us, length us, event | category | flops | bytes accessed | tf_op | source)
XLA Modules:
  0.0 90.6 jit_solution(14365091431962326233)
XLA Ops:
  0.6 27.5 %exchange.1 = (f32[192,32768]{1,0:T(8,128)S(1)}, f32[192,32768]{1,0:T(8,128)S(1)}, f32[2,18,8,8192]{3,2,1,0:T(8,128)S(1)}, bf16[12,8,16384]{2,1,0:T(8,128)(2,1)S...) custom-call(bf16[1,192,65536]{2,1,0:T(8,128)(2,1)} %grads.1, f32[192,32768]{1,0:T(8,128)} %master.1, ...), custom_call_target="tpu_custom_call" | custom-call | tf_op jit(solution)/shard_map/exchange/pallas_call | solution.py:489
  28.1 31.2 %moments.1 = (f32[192,32768]{1,0:T(8,128)S(1)}, f32[192,32768]{1,0:T(8,128)S(1)}, f32[2,18,8,8192]{3,2,1,0:T(8,128)S(1)}, bf16[12,8,16384]{2,1,0:T(8,128)(2,1)S(...) custom-call(f32[192,32768]{1,0:T(8,128)S(1)} %get-tuple-element.20.m, ...), custom_call_target="tpu_custom_call", output_to_operand_aliasing={{0}: (0, {}), {1}: (1, {}), {2}: (2, {}), {3}: (3, {})} | custom-call | tf_op jit(solution)/shard_map/moments/pallas_call | solution.py:500
  59.3 13.8 %weights.1 = (bf16[7,8,32768]{2,1,0:T(8,128)(2,1)S(1)}, f32[2,8,128]{2,1,0:T(8,128)S(1)}, bf16[17,8,32768]{2,1,0:T(8,128)(2,1)}) custom-call(f32[192,32768]{1,0:T(8,128)S(1)} %get-tuple-element.26.direction, f32[192,32768]{1,0:T(8,128)S(1)} %get-tuple-element.27.weight, f32[2,8,128]{2,1,0:T(8,128)S(1)} %get-tuple-element.28.stats), custom_call_target="tpu_custom_call", output_to_operand_aliasing={{1}: (2, {})} | custom-call | tf_op jit(solution)/shard_map/weights/pallas_call | solution.py:511
  73.1 0.1 collective-permute-start
  73.3 13.7 %write.1 = (bf16[192,65536]{1,0:T(8,128)(2,1)}, f32[192,32768]{1,0:T(8,128)}) custom-call(f32[192,32768]{1,0:T(8,128)S(1)} %get-tuple-element.26.direction, f32[192,32768]{1,0:T(8,128)S(1)} %get-tuple-element.27.weight, bf16[7,8,32768]{2,1,0:T(8,128)(2,1)S(1)} %get-tuple-element.30.land, f32[2,8,128]{2,1,0:T(8,128)S(1)} %get-tuple-element.31.rate), custom_call_target="tpu_custom_call" | custom-call | tf_op jit(solution)/shard_map/write/pallas_call | solution.py:525
  86.9 0.1 collective-permute-done.given
  87.1 3.6 %place.1 = bf16[192,65536]{1,0:T(8,128)(2,1)} custom-call(bf16[17,8,32768]{2,1,0:T(8,128)(2,1)S(1)} %collective-permute-done.given, bf16[192,65536]{1,0:T(8,128)(2,1)} %get-tuple-element.32.params_in), custom_call_target="tpu_custom_call", output_to_operand_aliasing={{}: (1, {})} | custom-call | tf_op jit(solution)/shard_map/place/pallas_call | solution.py:535
Async XLA Ops:
  73.1 13.9 %collective-permute-start = (bf16[17,8,32768]{2,1,0:T(8,128)(2,1)}, bf16[17,8,32768]{2,1,0:T(8,128)(2,1)S(1)}, u32[]{:S(2)}, u32[]{:S(2)}) collective-permute-start(bf16[17,8,32768]{2,1,0:T(8,128)(2,1)} %get-tuple-element.29), channel_id=1, source_target_pairs={{0,1},{1,0},{2,3},{3,2},{4,5},{5,4},{6,7},{7,6}} | collective-permute-start | bytes 26738696 | tf_op jit(solution)/shard_map/ppermute | solution.py:523

commit v10 on v9

--- a/solution.py
+++ b/solution.py
@@ -29,15 +29,16 @@
 AHEAD = 4
 LAND_SLOTS = 8
 STAGE_SLOTS = 12
-OWN_SLOTS = 7
+OWN_SLOTS = 6
 RING = 18
 LAG = 7
 MOMENT_WIDTH = 4096
-MEAN_WIDTH = 2048
+MEAN_WIDTH = 4096
+PACK_WIDTH = 4096
 CHUNK = 8192
 SEND_SLOTS = 3
 RIDE = 17
-RIDE_SLOTS = 4
+RIDE_SLOTS = 3
 WRITE_SLOTS = 5
 WRITE_CHUNK = 16384
 
@@ -53,6 +54,11 @@
 def put_lane(tile, lane_ids, lane, partial):
     row_sum = jnp.sum(partial, axis=1, keepdims=True)
     return tile + jnp.where(lane_ids == lane, row_sum, 0.0)
+
+
+def swap(values):
+    parts = [values[:, at:at + LANES] for at in range(0, values.shape[1], LANES)]
+    return jnp.concatenate([parts[index ^ 1] for index in range(len(parts))], axis=1)
 
 
 def tree_sum(values):
@@ -171,7 +177,7 @@
             far = pl.ds(pl.multiple_of(col_at + step * width, width), width)
             weight = weight_ref[row_at, far]
             mean = (own[own_slot, :, near].astype(F32) + land[land_slot, :, near].astype(F32)) * 0.5
-            mean_ref[row_at, far] = mean
+            mean_ref[row_at, far] = swap(mean)
             cuts = range(0, width, LANES)
             grad_sum += tree_sum([mean[:, at:at + LANES] * mean[:, at:at + LANES] for at in cuts])
             weight_sum += tree_sum([weight[:, at:at + LANES] * weight[:, at:at + LANES] for at in cuts])
@@ -265,7 +271,7 @@
         def piece(index, total):
             near = pl.ds(pl.multiple_of(index * width, width), width)
             far = pl.ds(pl.multiple_of(col_at + index * width, width), width)
-            mean, weight = dir_ref[row_at, far], weight_ref[row_at, far]
+            mean, weight = swap(dir_ref[row_at, far]), weight_ref[row_at, far]
             old_one, old_two = ring[0, slot, :, near], ring[1, slot, :, near]
             new_one = BETA_ONE * old_one + one_scale * mean
             new_two = BETA_TWO * old_two + two_scale * mean * mean
@@ -273,7 +279,7 @@
             direction = (new_one * ratio) / (root + floor) + WEIGHT_DECAY * weight
             ring[0, slot, :, near] = new_one
             ring[1, slot, :, near] = new_two
-            dir_ref[row_at, far] = direction
+            dir_ref[row_at, far] = swap(direction)
             return total + tree_sum([direction[:, at:at + LANES] * direction[:, at:at + LANES] for at in range(0, width, LANES)])
 
         total = lax.fori_loop(0, CHUNK // width, piece, jnp.zeros((GROUP, LANES), F32))
@@ -324,7 +330,7 @@
     dir_sq = segment_sums(tree_sum([slots[index, 0] for index in range(model_size * data_size)]))
     weight_sq = segment_sums(tree_sum([slots[index, 1] for index in range(model_size * data_size)]))
     rate[0] = LEARN_RATE * (jnp.sqrt(weight_sq) / jnp.sqrt(dir_sq))
-    width = 1024
+    width = PACK_WIDTH
 
     def send_copy(group):
         slot = lax.rem(group, SEND_SLOTS)
@@ -340,10 +346,10 @@
 
         def piece(index, inner):
             at = pl.ds(pl.multiple_of(index * width, width), width)
-            target[slot, :, at] = (weight[rows(group), at] - group_rate * direction[rows(group), at]).astype(BF16)
+            target[slot, :, at] = (weight[rows(group), at] - group_rate * swap(direction[rows(group), at])).astype(BF16)
             return inner
 
-        lax.fori_loop(0, cols // width, piece, 0, unroll=2)
+        lax.fori_loop(0, cols // width, piece, 0)
 
     def one_group(group, carry):
         slot = lax.rem(group, SEND_SLOTS)
@@ -384,7 +390,7 @@
     data_size = sizes[1]
     data = lax.axis_index('data')
     peer = lax.rem(data + 1, data_size)
-    width = 1024
+    width = PACK_WIDTH
     lane_ids = lanes_of()
     per_group = cols // WRITE_CHUNK
     chunks = groups * per_group
@@ -419,12 +425,12 @@
         def piece(index, inner):
             near = pl.ds(pl.multiple_of(index * width, width), width)
             far = pl.ds(pl.multiple_of(lax.rem(chunk, per_group) * WRITE_CHUNK + index * width, width), width)
-            new = weight[rows(group), far] - group_rate * direction[rows(group), far]
+            new = weight[rows(group), far] - group_rate * swap(direction[rows(group), far])
             fresh[slot, :, near] = new
             packed[slot, :, near] = new.astype(BF16)
             return inner
 
-        lax.fori_loop(0, WRITE_CHUNK // width, piece, 0, unroll=2)
+        lax.fori_loop(0, WRITE_CHUNK // width, piece, 0)
         for priority, copy in enumerate(puts(chunk)):
             copy.start(priority=priority)
         return carry

time: 90.7 us -> 89.2 us (0.983)
  Pallas kernels: 89.7 us -> 88.1 us
    pallas_call x1, Pallas kernels: 13.8 us -> 12.2 us  [device_step(): pl.pallas_call(functools.partial(weight_kernel, sizes, groups, cols), out...]
  transfers between devices with their start and end apart: 1 -> 1, of which waited for: 1 -> 0; matrix products, arithmetic and copies ran while one was open for 0% -> 0% of each run, Pallas kernels for 15% -> 15%
where the time goes in v10:
time: 89.2 us; the launch traced here: 89.1 us
  Pallas kernels  88.1 us (99%)
    pallas_call x1, Pallas kernels, device_step(): pl.pallas_call(functools.partial(moment_kernel, groups, cols), out_shape=...  31.2 us
    pallas_call x1, Pallas kernels, device_step(): pl.pallas_call(functools.partial(exchange_kernel, sizes, groups, cols), o...  27.4 us
    pallas_call x1, Pallas kernels, device_step(): pl.pallas_call(functools.partial(write_kernel, sizes, groups, cols), out_...  13.7 us
    pallas_call x1, Pallas kernels, device_step(): pl.pallas_call(functools.partial(weight_kernel, sizes, groups, cols), out...  12.2 us
    pallas_call x1, Pallas kernels, device_step(): pl.pallas_call(functools.partial(place_kernel, sizes, groups, cols), out_...  3.6 us
  transfers between devices with their start and end apart: 1, of which 0 were waited for; matrix products, arithmetic and copies ran while one was open for 0% of the time, Pallas kernels for 15%

profile of v10, /device:TPU:0, one launch (start us, length us, event | category | flops | bytes accessed | tf_op | source)
XLA Modules:
  0.0 89.1 jit_solution(7190328606482801866)
XLA Ops:
  0.6 27.4 %exchange.1 = (f32[192,32768]{1,0:T(8,128)S(1)}, f32[192,32768]{1,0:T(8,128)S(1)}, f32[2,18,8,8192]{3,2,1,0:T(8,128)S(1)}, bf16[12,8,16384]{2,1,0:T(8,128)(2,1)S...) custom-call(bf16[1,192,65536]{2,1,0:T(8,128)(2,1)} %grads.1, f32[192,32768]{1,0:T(8,128)} %master.1, ...), custom_call_target="tpu_custom_call" | custom-call | tf_op jit(solution)/shard_map/exchange/pallas_call | solution.py:495
  28.0 31.2 %moments.1 = (f32[192,32768]{1,0:T(8,128)S(1)}, f32[192,32768]{1,0:T(8,128)S(1)}, f32[2,18,8,8192]{3,2,1,0:T(8,128)S(1)}, bf16[12,8,16384]{2,1,0:T(8,128)(2,1)S(...) custom-call(f32[192,32768]{1,0:T(8,128)S(1)} %get-tuple-element.20.m, ...), custom_call_target="tpu_custom_call", output_to_operand_aliasing={{0}: (0, {}), {1}: (1, {}), {2}: (2, {}), {3}: (3, {})} | custom-call | tf_op jit(solution)/shard_map/moments/pallas_call | solution.py:506
  59.2 12.2 %weights.1 = (bf16[7,8,32768]{2,1,0:T(8,128)(2,1)S(1)}, f32[2,8,128]{2,1,0:T(8,128)S(1)}, bf16[17,8,32768]{2,1,0:T(8,128)(2,1)}) custom-call(f32[192,32768]{1,0:T(8,128)S(1)} %get-tuple-element.26.direction, f32[192,32768]{1,0:T(8,128)S(1)} %get-tuple-element.27.weight, f32[2,8,128]{2,1,0:T(8,128)S(1)} %get-tuple-element.28.stats), custom_call_target="tpu_custom_call", output_to_operand_aliasing={{1}: (2, {})} | custom-call | tf_op jit(solution)/shard_map/weights/pallas_call | solution.py:517
  71.4 0.3 collective-permute-start
  71.7 13.7 %write.1 = (bf16[192,65536]{1,0:T(8,128)(2,1)}, f32[192,32768]{1,0:T(8,128)}) custom-call(f32[192,32768]{1,0:T(8,128)S(1)} %get-tuple-element.26.direction, f32[192,32768]{1,0:T(8,128)S(1)} %get-tuple-element.27.weight, bf16[7,8,32768]{2,1,0:T(8,128)(2,1)S(1)} %get-tuple-element.30.land, f32[2,8,128]{2,1,0:T(8,128)S(1)} %get-tuple-element.31.rate), custom_call_target="tpu_custom_call" | custom-call | tf_op jit(solution)/shard_map/write/pallas_call | solution.py:531
  85.5 0.0 collective-permute-done.given
  85.5 3.6 %place.1 = bf16[192,65536]{1,0:T(8,128)(2,1)} custom-call(bf16[17,8,32768]{2,1,0:T(8,128)(2,1)S(1)} %collective-permute-done.given, bf16[192,65536]{1,0:T(8,128)(2,1)} %get-tuple-element.32.params_in), custom_call_target="tpu_custom_call", output_to_operand_aliasing={{}: (1, {})} | custom-call | tf_op jit(solution)/shard_map/place/pallas_call | solution.py:541
Async XLA Ops:
  71.4 14.0 %collective-permute-start = (bf16[17,8,32768]{2,1,0:T(8,128)(2,1)}, bf16[17,8,32768]{2,1,0:T(8,128)(2,1)S(1)}, u32[]{:S(2)}, u32[]{:S(2)}) collective-permute-start(bf16[17,8,32768]{2,1,0:T(8,128)(2,1)} %get-tuple-element.29), channel_id=1, source_target_pairs={{0,1},{1,0},{2,3},{3,2},{4,5},{5,4},{6,7},{7,6}} | collective-permute-start | bytes 26738696 | tf_op jit(solution)/shard_map/ppermute | solution.py:529

commit v11 on v10

--- a/solution.py
+++ b/solution.py
@@ -28,16 +28,16 @@
 PART = 16384
 AHEAD = 4
 LAND_SLOTS = 8
-STAGE_SLOTS = 12
+STAGE_SLOTS = 9
 OWN_SLOTS = 6
-RING = 18
-LAG = 7
+RING = 20
+LAG = 5
 MOMENT_WIDTH = 4096
-MEAN_WIDTH = 4096
-PACK_WIDTH = 4096
+MEAN_WIDTH = 2048
+PACK_WIDTH = 8192
 CHUNK = 8192
 SEND_SLOTS = 3
-RIDE = 17
+RIDE = 18
 RIDE_SLOTS = 3
 WRITE_SLOTS = 5
 WRITE_CHUNK = 16384
@@ -96,7 +96,7 @@
         copy.wait_send()
 
 
-def exchange_kernel(sizes, groups, cols, grads, master, one_in, two_in, mean_ref, weight_ref, ring, stage, clip_ref, stat_ref, land, own, part, slots,
+def exchange_kernel(sizes, groups, cols, grads, master, one_in, two_in, mean_ref, weight_ref, ring, land, clip_ref, stat_ref, stage, own, part, slots,
                     stage_sem, send_sem, recv_sem, free_sem, own_sem, weight_sem, ring_sem, small_send, small_recv):
     model_size, data_size = sizes
     data = lax.axis_index('data')
@@ -225,7 +225,7 @@
     lax.fori_loop(0, RING, finish, 0)
 
 
-def moment_kernel(groups, cols, mean_in, weight_in, ring_in, stage_in, clip, weight_stat, one_in, two_in, dir_ref, weight_ref, ring, stage, one_out, two_out, stat_ref,
+def moment_kernel(groups, cols, mean_in, weight_in, ring_in, land_in, clip, weight_stat, one_in, two_in, dir_ref, weight_ref, ring, land, one_out, two_out, stat_ref,
                   one_get, two_get, one_put, two_put):
     per_group = cols // CHUNK
     chunks = groups * per_group
@@ -390,7 +390,7 @@
     data_size = sizes[1]
     data = lax.axis_index('data')
     peer = lax.rem(data + 1, data_size)
-    width = PACK_WIDTH
+    width = 4096
     lane_ids = lanes_of()
     per_group = cols // WRITE_CHUNK
     chunks = groups * per_group
@@ -490,14 +490,14 @@
         riding = jax.ShapeDtypeStruct((RIDE, GROUP, cols), BF16)
         parts = groups * (cols // PART)
 
-        staged = pltpu.VMEM((STAGE_SLOTS, GROUP, PART), BF16)
-
-        mean, weight, ring, stage, clip, weight_stat = pl.pallas_call(
+        caught = pltpu.VMEM((LAND_SLOTS, GROUP, PART), BF16)
+
+        mean, weight, ring, catch, clip, weight_stat = pl.pallas_call(
             functools.partial(exchange_kernel, sizes, groups, cols),
-            out_shape=(kept, kept, ring_shape, staged, tile, tile),
+            out_shape=(kept, kept, ring_shape, caught, tile, tile),
             in_specs=[hbm] * 4,
             out_specs=[vmem] * 6,
-            scratch_shapes=[pltpu.VMEM((LAND_SLOTS, GROUP, PART), BF16), pltpu.VMEM((OWN_SLOTS, GROUP, PART), BF16), pltpu.VMEM((GROUP, LANES), F32), pltpu.VMEM((devices, GROUP, LANES), F32),
+            scratch_shapes=[pltpu.VMEM((STAGE_SLOTS, GROUP, PART), BF16), pltpu.VMEM((OWN_SLOTS, GROUP, PART), BF16), pltpu.VMEM((GROUP, LANES), F32), pltpu.VMEM((devices, GROUP, LANES), F32),
                             dma((STAGE_SLOTS,)), dma((STAGE_SLOTS,)), dma((LAND_SLOTS,)), pltpu.SemaphoreType.REGULAR, dma((OWN_SLOTS,)), dma((parts,)), dma((2, RING)), dma((devices,)), dma((devices,))],
             compiler_params=pltpu.CompilerParams(collective_id=0, has_side_effects=True, vmem_limit_bytes=SCOPE),
             name='exchange',
@@ -505,14 +505,14 @@
 
         direction, weight, _, _, new_one, new_two, stats = pl.pallas_call(
             functools.partial(moment_kernel, groups, cols),
-            out_shape=(kept, kept, ring_shape, staged, state, state, pltpu.VMEM((2, GROUP, LANES), F32)),
+            out_shape=(kept, kept, ring_shape, caught, state, state, pltpu.VMEM((2, GROUP, LANES), F32)),
             in_specs=[vmem] * 6 + [hbm] * 2,
             out_specs=[vmem, vmem, vmem, vmem, hbm, hbm, vmem],
             input_output_aliases={0: 0, 1: 1, 2: 2, 3: 3},
             scratch_shapes=[dma((RING,))] * 4,
             compiler_params=pltpu.CompilerParams(vmem_limit_bytes=SCOPE),
             name='moments',
-        )(mean, weight, ring, stage, keep(clip), keep(weight_stat), moment_one, moment_two)
+        )(mean, weight, ring, catch, keep(clip), keep(weight_stat), moment_one, moment_two)
 
         land, rate, ride = pl.pallas_call(
             functools.partial(weight_kernel, sizes, groups, cols),

time: 89.2 us -> 88.8 us (level)
  Pallas kernels: 88.1 us -> 87.1 us
  transfers between devices with their start and end apart: 1 -> 1, of which waited for: 0 -> 1; matrix products, arithmetic and copies ran while one was open for 0% -> 0% of each run, Pallas kernels for 15% -> 15%
where the time goes in v11:
time: 88.8 us; the launch traced here: 88.7 us
  Pallas kernels  87.1 us (98%)
    pallas_call x1, Pallas kernels, device_step(): pl.pallas_call(functools.partial(moment_kernel, groups, cols), out_shape=...  30.5 us
    pallas_call x1, Pallas kernels, device_step(): pl.pallas_call(functools.partial(exchange_kernel, sizes, groups, cols), o...  27.4 us
    pallas_call x1, Pallas kernels, device_step(): pl.pallas_call(functools.partial(write_kernel, sizes, groups, cols), out_...  13.7 us
    pallas_call x1, Pallas kernels, device_step(): pl.pallas_call(functools.partial(weight_kernel, sizes, groups, cols), out...  11.7 us
    pallas_call x1, Pallas kernels, device_step(): pl.pallas_call(functools.partial(place_kernel, sizes, groups, cols), out_...  3.75 us
  transfers between devices with their start and end apart: 1, of which 1 were waited for; matrix products, arithmetic and copies ran while one was open for 0% of the time, Pallas kernels for 15%

profile of v11, /device:TPU:0, one launch (start us, length us, event | category | flops | bytes accessed | tf_op | source)
XLA Modules:
  0.0 88.7 jit_solution(14228940298442131748)
XLA Ops:
  0.6 27.4 %exchange.1 = (f32[192,32768]{1,0:T(8,128)S(1)}, f32[192,32768]{1,0:T(8,128)S(1)}, f32[2,20,8,8192]{3,2,1,0:T(8,128)S(1)}, bf16[8,8,16384]{2,1,0:T(8,128)(2,1)S(...) custom-call(bf16[1,192,65536]{2,1,0:T(8,128)(2,1)} %grads.1, f32[192,32768]{1,0:T(8,128)} %master.1, f32[192,32768]{1,0:T(8,128)} %one_in.3, ...), custom_call_target="tpu_custom_call" | custom-call | tf_op jit(solution)/shard_map/exchange/pallas_call | solution.py:495
  28.0 30.5 %moments.1 = (f32[192,32768]{1,0:T(8,128)S(1)}, f32[192,32768]{1,0:T(8,128)S(1)}, f32[2,20,8,8192]{3,2,1,0:T(8,128)S(1)}, bf16[8,8,16384]{2,1,0:T(8,128)(2,1)S(1...) custom-call(f32[192,32768]{1,0:T(8,128)S(1)} %get-tuple-element.20.m, ...), custom_call_target="tpu_custom_call", output_to_operand_aliasing={{0}: (0, {}), {1}: (1, {}), {2}: (2, {}), {3}: (3, {})} | custom-call | tf_op jit(solution)/shard_map/moments/pallas_call | solution.py:506
  58.6 11.7 %weights.1 = (bf16[6,8,32768]{2,1,0:T(8,128)(2,1)S(1)}, f32[2,8,128]{2,1,0:T(8,128)S(1)}, bf16[18,8,32768]{2,1,0:T(8,128)(2,1)}) custom-call(f32[192,32768]{1,0:T(8,128)S(1)} %get-tuple-element.26.direction, f32[192,32768]{1,0:T(8,128)S(1)} %get-tuple-element.27.weight, f32[2,8,128]{2,1,0:T(8,128)S(1)} %get-tuple-element.28.stats), custom_call_target="tpu_custom_call", output_to_operand_aliasing={{1}: (2, {})} | custom-call | tf_op jit(solution)/shard_map/weights/pallas_call | solution.py:517
  70.3 0.4 collective-permute-start
  70.6 13.7 %write.1 = (bf16[192,65536]{1,0:T(8,128)(2,1)}, f32[192,32768]{1,0:T(8,128)}) custom-call(f32[192,32768]{1,0:T(8,128)S(1)} %get-tuple-element.26.direction, f32[192,32768]{1,0:T(8,128)S(1)} %get-tuple-element.27.weight, bf16[6,8,32768]{2,1,0:T(8,128)(2,1)S(1)} %get-tuple-element.30.land, f32[2,8,128]{2,1,0:T(8,128)S(1)} %get-tuple-element.31.rate), custom_call_target="tpu_custom_call" | custom-call | tf_op jit(solution)/shard_map/write/pallas_call | solution.py:531
  84.4 0.6 collective-permute-done.given
  85.0 3.7 %place.1 = bf16[192,65536]{1,0:T(8,128)(2,1)} custom-call(bf16[18,8,32768]{2,1,0:T(8,128)(2,1)S(1)} %collective-permute-done.given, bf16[192,65536]{1,0:T(8,128)(2,1)} %get-tuple-element.32.params_in), custom_call_target="tpu_custom_call", output_to_operand_aliasing={{}: (1, {})} | custom-call | tf_op jit(solution)/shard_map/place/pallas_call | solution.py:541
Async XLA Ops:
  70.3 14.7 %collective-permute-start = (bf16[18,8,32768]{2,1,0:T(8,128)(2,1)}, bf16[18,8,32768]{2,1,0:T(8,128)(2,1)S(1)}, u32[]{:S(2)}, u32[]{:S(2)}) collective-permute-start(bf16[18,8,32768]{2,1,0:T(8,128)(2,1)} %get-tuple-element.29), channel_id=1, source_target_pairs={{0,1},{1,0},{2,3},{3,2},{4,5},{5,4},{6,7},{7,6}} | collective-permute-start | bytes 28311560 | tf_op jit(solution)/shard_map/ppermute | solution.py:529

commit v12 on v11

--- a/solution.py
+++ b/solution.py
@@ -31,14 +31,14 @@
 STAGE_SLOTS = 9
 OWN_SLOTS = 6
 RING = 20
-LAG = 5
+LAG = 3
 MOMENT_WIDTH = 4096
 MEAN_WIDTH = 2048
 PACK_WIDTH = 8192
 CHUNK = 8192
-SEND_SLOTS = 3
-RIDE = 18
-RIDE_SLOTS = 3
+SEND_SLOTS = 2
+RIDE = 17
+RIDE_SLOTS = 4
 WRITE_SLOTS = 5
 WRITE_CHUNK = 16384
 

time: 88.8 us -> 88.4 us (level)
  transfers between devices with their start and end apart: 1 -> 1, of which waited for: 1 -> 0; matrix products, arithmetic and copies ran while one was open for 0% -> 0% of each run, Pallas kernels for 15% -> 16%
where the time goes in v12:
time: 88.4 us
  Pallas kernels  87.3 us (99%)
    pallas_call x1, Pallas kernels, device_step(): pl.pallas_call(functools.partial(moment_kernel, groups, cols), out_shape=...  30.5 us
    pallas_call x1, Pallas kernels, device_step(): pl.pallas_call(functools.partial(exchange_kernel, sizes, groups, cols), o...  27.4 us
    pallas_call x1, Pallas kernels, device_step(): pl.pallas_call(functools.partial(write_kernel, sizes, groups, cols), out_...  13.7 us
    pallas_call x1, Pallas kernels, device_step(): pl.pallas_call(functools.partial(weight_kernel, sizes, groups, cols), out...  12 us
    pallas_call x1, Pallas kernels, device_step(): pl.pallas_call(functools.partial(place_kernel, sizes, groups, cols), out_...  3.6 us
  transfers between devices with their start and end apart: 1, of which 0 were waited for; matrix products, arithmetic and copies ran while one was open for 0% of the time, Pallas kernels for 16%

profile of v12, /device:TPU:0, one launch (start us, length us, event | category | flops | bytes accessed | tf_op | source)
XLA Modules:
  0.0 88.4 jit_solution(11596879574324654086)
XLA Ops:
  0.6 27.4 %exchange.1 = (f32[192,32768]{1,0:T(8,128)S(1)}, f32[192,32768]{1,0:T(8,128)S(1)}, f32[2,20,8,8192]{3,2,1,0:T(8,128)S(1)}, bf16[8,8,16384]{2,1,0:T(8,128)(2,1)S(...) custom-call(bf16[1,192,65536]{2,1,0:T(8,128)(2,1)} %grads.1, f32[192,32768]{1,0:T(8,128)} %master.1, f32[192,32768]{1,0:T(8,128)} %one_in.3, ...), custom_call_target="tpu_custom_call" | custom-call | tf_op jit(solution)/shard_map/exchange/pallas_call | solution.py:495
  28.0 30.5 %moments.1 = (f32[192,32768]{1,0:T(8,128)S(1)}, f32[192,32768]{1,0:T(8,128)S(1)}, f32[2,20,8,8192]{3,2,1,0:T(8,128)S(1)}, bf16[8,8,16384]{2,1,0:T(8,128)(2,1)S(1...) custom-call(f32[192,32768]{1,0:T(8,128)S(1)} %get-tuple-element.20.m, ...), custom_call_target="tpu_custom_call", output_to_operand_aliasing={{0}: (0, {}), {1}: (1, {}), {2}: (2, {}), {3}: (3, {})} | custom-call | tf_op jit(solution)/shard_map/moments/pallas_call | solution.py:506
  58.6 12.0 %weights.1 = (bf16[7,8,32768]{2,1,0:T(8,128)(2,1)S(1)}, f32[2,8,128]{2,1,0:T(8,128)S(1)}, bf16[17,8,32768]{2,1,0:T(8,128)(2,1)}) custom-call(f32[192,32768]{1,0:T(8,128)S(1)} %get-tuple-element.26.direction, f32[192,32768]{1,0:T(8,128)S(1)} %get-tuple-element.27.weight, f32[2,8,128]{2,1,0:T(8,128)S(1)} %get-tuple-element.28.stats), custom_call_target="tpu_custom_call", output_to_operand_aliasing={{1}: (2, {})} | custom-call | tf_op jit(solution)/shard_map/weights/pallas_call | solution.py:517
  70.6 0.4 collective-permute-start
  71.0 13.7 %write.1 = (bf16[192,65536]{1,0:T(8,128)(2,1)}, f32[192,32768]{1,0:T(8,128)}) custom-call(f32[192,32768]{1,0:T(8,128)S(1)} %get-tuple-element.26.direction, f32[192,32768]{1,0:T(8,128)S(1)} %get-tuple-element.27.weight, bf16[7,8,32768]{2,1,0:T(8,128)(2,1)S(1)} %get-tuple-element.30.land, f32[2,8,128]{2,1,0:T(8,128)S(1)} %get-tuple-element.31.rate), custom_call_target="tpu_custom_call" | custom-call | tf_op jit(solution)/shard_map/write/pallas_call | solution.py:531
  84.7 0.0 collective-permute-done.given
  84.8 3.6 %place.1 = bf16[192,65536]{1,0:T(8,128)(2,1)} custom-call(bf16[17,8,32768]{2,1,0:T(8,128)(2,1)S(1)} %collective-permute-done.given, bf16[192,65536]{1,0:T(8,128)(2,1)} %get-tuple-element.32.params_in), custom_call_target="tpu_custom_call", output_to_operand_aliasing={{}: (1, {})} | custom-call | tf_op jit(solution)/shard_map/place/pallas_call | solution.py:541
Async XLA Ops:
  70.6 14.1 %collective-permute-start = (bf16[17,8,32768]{2,1,0:T(8,128)(2,1)}, bf16[17,8,32768]{2,1,0:T(8,128)(2,1)S(1)}, u32[]{:S(2)}, u32[]{:S(2)}) collective-permute-start(bf16[17,8,32768]{2,1,0:T(8,128)(2,1)} %get-tuple-element.29), channel_id=1, source_target_pairs={{0,1},{1,0},{2,3},{3,2},{4,5},{5,4},{6,7},{7,6}} | collective-permute-start | bytes 26738696 | tf_op jit(solution)/shard_map/ppermute | solution.py:529

commit v13 on v12

--- a/solution.py
+++ b/solution.py
@@ -31,12 +31,12 @@
 STAGE_SLOTS = 9
 OWN_SLOTS = 6
 RING = 20
-LAG = 3
-MOMENT_WIDTH = 4096
+LAG = 4
+MOMENT_WIDTH = 8192
 MEAN_WIDTH = 2048
 PACK_WIDTH = 8192
 CHUNK = 8192
-SEND_SLOTS = 2
+SEND_SLOTS = 3
 RIDE = 17
 RIDE_SLOTS = 4
 WRITE_SLOTS = 5

time: 88.4 us -> 87.6 us (level)
  no operation moved by 1% of the time
where the time goes in v13:
time: 87.6 us
  Pallas kernels  86.5 us (99%)
    pallas_call x1, Pallas kernels, device_step(): pl.pallas_call(functools.partial(moment_kernel, groups, cols), out_shape=...  30.4 us
    pallas_call x1, Pallas kernels, device_step(): pl.pallas_call(functools.partial(exchange_kernel, sizes, groups, cols), o...  27.4 us
    pallas_call x1, Pallas kernels, device_step(): pl.pallas_call(functools.partial(write_kernel, sizes, groups, cols), out_...  13.7 us
    pallas_call x1, Pallas kernels, device_step(): pl.pallas_call(functools.partial(weight_kernel, sizes, groups, cols), out...  11.3 us
    pallas_call x1, Pallas kernels, device_step(): pl.pallas_call(functools.partial(place_kernel, sizes, groups, cols), out_...  3.6 us
  transfers between devices with their start and end apart: 1, of which 0 were waited for; matrix products, arithmetic and copies ran while one was open for 0% of the time, Pallas kernels for 16%

profile of v13, /device:TPU:0, one launch (start us, length us, event | category | flops | bytes accessed | tf_op | source)
XLA Modules:
  0.0 87.6 jit_solution(17436081123072485584)
XLA Ops:
  0.6 27.4 %exchange.1 = (f32[192,32768]{1,0:T(8,128)S(1)}, f32[192,32768]{1,0:T(8,128)S(1)}, f32[2,20,8,8192]{3,2,1,0:T(8,128)S(1)}, bf16[8,8,16384]{2,1,0:T(8,128)(2,1)S(...) custom-call(bf16[1,192,65536]{2,1,0:T(8,128)(2,1)} %grads.1, f32[192,32768]{1,0:T(8,128)} %master.1, f32[192,32768]{1,0:T(8,128)} %one_in.3, ...), custom_call_target="tpu_custom_call" | custom-call | tf_op jit(solution)/shard_map/exchange/pallas_call | solution.py:495
  28.0 30.4 %moments.1 = (f32[192,32768]{1,0:T(8,128)S(1)}, f32[192,32768]{1,0:T(8,128)S(1)}, f32[2,20,8,8192]{3,2,1,0:T(8,128)S(1)}, bf16[8,8,16384]{2,1,0:T(8,128)(2,1)S(1...) custom-call(f32[192,32768]{1,0:T(8,128)S(1)} %get-tuple-element.20.m, ...), custom_call_target="tpu_custom_call", output_to_operand_aliasing={{0}: (0, {}), {1}: (1, {}), {2}: (2, {}), {3}: (3, {})} | custom-call | tf_op jit(solution)/shard_map/moments/pallas_call | solution.py:506
  58.5 11.3 %weights.1 = (bf16[7,8,32768]{2,1,0:T(8,128)(2,1)S(1)}, f32[2,8,128]{2,1,0:T(8,128)S(1)}, bf16[17,8,32768]{2,1,0:T(8,128)(2,1)}) custom-call(f32[192,32768]{1,0:T(8,128)S(1)} %get-tuple-element.26.direction, f32[192,32768]{1,0:T(8,128)S(1)} %get-tuple-element.27.weight, f32[2,8,128]{2,1,0:T(8,128)S(1)} %get-tuple-element.28.stats), custom_call_target="tpu_custom_call", output_to_operand_aliasing={{1}: (2, {})} | custom-call | tf_op jit(solution)/shard_map/weights/pallas_call | solution.py:517
  69.8 0.4 collective-permute-start
  70.2 13.7 %write.1 = (bf16[192,65536]{1,0:T(8,128)(2,1)}, f32[192,32768]{1,0:T(8,128)}) custom-call(f32[192,32768]{1,0:T(8,128)S(1)} %get-tuple-element.26.direction, f32[192,32768]{1,0:T(8,128)S(1)} %get-tuple-element.27.weight, bf16[7,8,32768]{2,1,0:T(8,128)(2,1)S(1)} %get-tuple-element.30.land, f32[2,8,128]{2,1,0:T(8,128)S(1)} %get-tuple-element.31.rate), custom_call_target="tpu_custom_call" | custom-call | tf_op jit(solution)/shard_map/write/pallas_call | solution.py:531
  83.9 0.0 collective-permute-done.given
  84.0 3.6 %place.1 = bf16[192,65536]{1,0:T(8,128)(2,1)} custom-call(bf16[17,8,32768]{2,1,0:T(8,128)(2,1)S(1)} %collective-permute-done.given, bf16[192,65536]{1,0:T(8,128)(2,1)} %get-tuple-element.32.params_in), custom_call_target="tpu_custom_call", output_to_operand_aliasing={{}: (1, {})} | custom-call | tf_op jit(solution)/shard_map/place/pallas_call | solution.py:541
Async XLA Ops:
  69.8 14.1 %collective-permute-start = (bf16[17,8,32768]{2,1,0:T(8,128)(2,1)}, bf16[17,8,32768]{2,1,0:T(8,128)(2,1)S(1)}, u32[]{:S(2)}, u32[]{:S(2)}) collective-permute-start(bf16[17,8,32768]{2,1,0:T(8,128)(2,1)} %get-tuple-element.29), channel_id=1, source_target_pairs={{0,1},{1,0},{2,3},{3,2},{4,5},{5,4},{6,7},{7,6}} | collective-permute-start | bytes 26738696 | tf_op jit(solution)/shard_map/ppermute | solution.py:529

commit v14 on v13

--- a/solution.py
+++ b/solution.py
@@ -26,7 +26,7 @@
 GROUP = 8
 
 PART = 16384
-AHEAD = 4
+AHEAD = 6
 LAND_SLOTS = 8
 STAGE_SLOTS = 9
 OWN_SLOTS = 6
@@ -289,7 +289,8 @@
         @pl.when(jnp.logical_and(ahead >= RING, ahead < chunks))
         def _():
             wait(puts(ahead - RING))
-            start(gets(ahead))
+            for priority, copy in enumerate(gets(ahead)):
+                copy.start(priority=priority)
 
         return put_lane(stat, lane_ids, chunk // per_group, total)
 

time: 87.6 us -> 95.2 us (1.087)
  Pallas kernels: 86.5 us -> 93.6 us
    pallas_call x1, Pallas kernels: 27.4 us -> 33.3 us  [device_step(): pl.pallas_call(functools.partial(exchange_kernel, sizes, groups, cols), o...]
    pallas_call x1, Pallas kernels: 30.4 us -> 31.7 us  [device_step(): pl.pallas_call(functools.partial(moment_kernel, groups, cols), out_shape=...]
  transfers between devices with their start and end apart: 1 -> 1, of which waited for: 0 -> 0; matrix products, arithmetic and copies ran while one was open for 0% -> 0% of each run, Pallas kernels for 16% -> 15%
where the time goes in v14:
time: 95.2 us; the launch traced here: 94.7 us
  Pallas kernels  93.6 us (98%)
    pallas_call x1, Pallas kernels, device_step(): pl.pallas_call(functools.partial(exchange_kernel, sizes, groups, cols), o...  33.3 us
    pallas_call x1, Pallas kernels, device_step(): pl.pallas_call(functools.partial(moment_kernel, groups, cols), out_shape=...  31.7 us
    pallas_call x1, Pallas kernels, device_step(): pl.pallas_call(functools.partial(write_kernel, sizes, groups, cols), out_...  13.7 us
    pallas_call x1, Pallas kernels, device_step(): pl.pallas_call(functools.partial(weight_kernel, sizes, groups, cols), out...  11.3 us
    pallas_call x1, Pallas kernels, device_step(): pl.pallas_call(functools.partial(place_kernel, sizes, groups, cols), out_...  3.6 us
  transfers between devices with their start and end apart: 1, of which 0 were waited for; matrix products, arithmetic and copies ran while one was open for 0% of the time, Pallas kernels for 15%

profile of v14, /device:TPU:0, one launch (start us, length us, event | category | flops | bytes accessed | tf_op | source)
XLA Modules:
  0.0 94.7 jit_solution(8729926216330539004)
XLA Ops:
  0.6 33.3 %exchange.1 = (f32[192,32768]{1,0:T(8,128)S(1)}, f32[192,32768]{1,0:T(8,128)S(1)}, f32[2,20,8,8192]{3,2,1,0:T(8,128)S(1)}, bf16[8,8,16384]{2,1,0:T(8,128)(2,1)S(...) custom-call(bf16[1,192,65536]{2,1,0:T(8,128)(2,1)} %grads.1, f32[192,32768]{1,0:T(8,128)} %master.1, f32[192,32768]{1,0:T(8,128)} %one_in.3, ...), custom_call_target="tpu_custom_call" | custom-call | tf_op jit(solution)/shard_map/exchange/pallas_call | solution.py:496
  34.0 31.7 %moments.1 = (f32[192,32768]{1,0:T(8,128)S(1)}, f32[192,32768]{1,0:T(8,128)S(1)}, f32[2,20,8,8192]{3,2,1,0:T(8,128)S(1)}, bf16[8,8,16384]{2,1,0:T(8,128)(2,1)S(1...) custom-call(f32[192,32768]{1,0:T(8,128)S(1)} %get-tuple-element.20.m, ...), custom_call_target="tpu_custom_call", output_to_operand_aliasing={{0}: (0, {}), {1}: (1, {}), {2}: (2, {}), {3}: (3, {})} | custom-call | tf_op jit(solution)/shard_map/moments/pallas_call | solution.py:507
  65.6 11.3 %weights.1 = (bf16[7,8,32768]{2,1,0:T(8,128)(2,1)S(1)}, f32[2,8,128]{2,1,0:T(8,128)S(1)}, bf16[17,8,32768]{2,1,0:T(8,128)(2,1)}) custom-call(f32[192,32768]{1,0:T(8,128)S(1)} %get-tuple-element.26.direction, f32[192,32768]{1,0:T(8,128)S(1)} %get-tuple-element.27.weight, f32[2,8,128]{2,1,0:T(8,128)S(1)} %get-tuple-element.28.stats), custom_call_target="tpu_custom_call", output_to_operand_aliasing={{1}: (2, {})} | custom-call | tf_op jit(solution)/shard_map/weights/pallas_call | solution.py:518
  77.0 0.4 collective-permute-start
  77.4 13.7 %write.1 = (bf16[192,65536]{1,0:T(8,128)(2,1)}, f32[192,32768]{1,0:T(8,128)}) custom-call(f32[192,32768]{1,0:T(8,128)S(1)} %get-tuple-element.26.direction, f32[192,32768]{1,0:T(8,128)S(1)} %get-tuple-element.27.weight, bf16[7,8,32768]{2,1,0:T(8,128)(2,1)S(1)} %get-tuple-element.30.land, f32[2,8,128]{2,1,0:T(8,128)S(1)} %get-tuple-element.31.rate), custom_call_target="tpu_custom_call" | custom-call | tf_op jit(solution)/shard_map/write/pallas_call | solution.py:532
  91.1 0.0 collective-permute-done.given
  91.1 3.6 %place.1 = bf16[192,65536]{1,0:T(8,128)(2,1)} custom-call(bf16[17,8,32768]{2,1,0:T(8,128)(2,1)S(1)} %collective-permute-done.given, bf16[192,65536]{1,0:T(8,128)(2,1)} %get-tuple-element.32.params_in), custom_call_target="tpu_custom_call", output_to_operand_aliasing={{}: (1, {})} | custom-call | tf_op jit(solution)/shard_map/place/pallas_call | solution.py:542
Async XLA Ops:
  77.0 14.1 %collective-permute-start = (bf16[17,8,32768]{2,1,0:T(8,128)(2,1)}, bf16[17,8,32768]{2,1,0:T(8,128)(2,1)S(1)}, u32[]{:S(2)}, u32[]{:S(2)}) collective-permute-start(bf16[17,8,32768]{2,1,0:T(8,128)(2,1)} %get-tuple-element.29), channel_id=1, source_target_pairs={{0,1},{1,0},{2,3},{3,2},{4,5},{5,4},{6,7},{7,6}} | collective-permute-start | bytes 26738696 | tf_op jit(solution)/shard_map/ppermute | solution.py:530

commit v15 on v13

--- a/solution.py
+++ b/solution.py
@@ -26,10 +26,10 @@
 GROUP = 8
 
 PART = 16384
-AHEAD = 4
+AHEAD = 5
 LAND_SLOTS = 8
-STAGE_SLOTS = 9
-OWN_SLOTS = 6
+STAGE_SLOTS = 10
+OWN_SLOTS = 5
 RING = 20
 LAG = 4
 MOMENT_WIDTH = 8192

time: 87.6 us -> 88 us (level)
  no operation moved by 1% of the time
where the time goes in v15:
time: 88 us; the launch traced here: 87.9 us
  Pallas kernels  86.8 us (99%)
    pallas_call x1, Pallas kernels, device_step(): pl.pallas_call(functools.partial(moment_kernel, groups, cols), out_shape=...  30.4 us
    pallas_call x1, Pallas kernels, device_step(): pl.pallas_call(functools.partial(exchange_kernel, sizes, groups, cols), o...  27.7 us
    pallas_call x1, Pallas kernels, device_step(): pl.pallas_call(functools.partial(write_kernel, sizes, groups, cols), out_...  13.7 us
    pallas_call x1, Pallas kernels, device_step(): pl.pallas_call(functools.partial(weight_kernel, sizes, groups, cols), out...  11.3 us
    pallas_call x1, Pallas kernels, device_step(): pl.pallas_call(functools.partial(place_kernel, sizes, groups, cols), out_...  3.6 us
  transfers between devices with their start and end apart: 1, of which 0 were waited for; matrix products, arithmetic and copies ran while one was open for 0% of the time, Pallas kernels for 16%

profile of v15, /device:TPU:0, one launch (start us, length us, event | category | flops | bytes accessed | tf_op | source)
XLA Modules:
  0.0 87.9 jit_solution(1834761240404731290)
XLA Ops:
  0.6 27.7 %exchange.1 = (f32[192,32768]{1,0:T(8,128)S(1)}, f32[192,32768]{1,0:T(8,128)S(1)}, f32[2,20,8,8192]{3,2,1,0:T(8,128)S(1)}, bf16[8,8,16384]{2,1,0:T(8,128)(2,1)S(...) custom-call(bf16[1,192,65536]{2,1,0:T(8,128)(2,1)} %grads.1, f32[192,32768]{1,0:T(8,128)} %master.1, f32[192,32768]{1,0:T(8,128)} %one_in.3, ...), custom_call_target="tpu_custom_call" | custom-call | tf_op jit(solution)/shard_map/exchange/pallas_call | solution.py:495
  28.4 30.4 %moments.1 = (f32[192,32768]{1,0:T(8,128)S(1)}, f32[192,32768]{1,0:T(8,128)S(1)}, f32[2,20,8,8192]{3,2,1,0:T(8,128)S(1)}, bf16[8,8,16384]{2,1,0:T(8,128)(2,1)S(1...) custom-call(f32[192,32768]{1,0:T(8,128)S(1)} %get-tuple-element.20.m, ...), custom_call_target="tpu_custom_call", output_to_operand_aliasing={{0}: (0, {}), {1}: (1, {}), {2}: (2, {}), {3}: (3, {})} | custom-call | tf_op jit(solution)/shard_map/moments/pallas_call | solution.py:506
  58.8 11.3 %weights.1 = (bf16[7,8,32768]{2,1,0:T(8,128)(2,1)S(1)}, f32[2,8,128]{2,1,0:T(8,128)S(1)}, bf16[17,8,32768]{2,1,0:T(8,128)(2,1)}) custom-call(f32[192,32768]{1,0:T(8,128)S(1)} %get-tuple-element.26.direction, f32[192,32768]{1,0:T(8,128)S(1)} %get-tuple-element.27.weight, f32[2,8,128]{2,1,0:T(8,128)S(1)} %get-tuple-element.28.stats), custom_call_target="tpu_custom_call", output_to_operand_aliasing={{1}: (2, {})} | custom-call | tf_op jit(solution)/shard_map/weights/pallas_call | solution.py:517
  70.2 0.4 collective-permute-start
  70.6 13.7 %write.1 = (bf16[192,65536]{1,0:T(8,128)(2,1)}, f32[192,32768]{1,0:T(8,128)}) custom-call(f32[192,32768]{1,0:T(8,128)S(1)} %get-tuple-element.26.direction, f32[192,32768]{1,0:T(8,128)S(1)} %get-tuple-element.27.weight, bf16[7,8,32768]{2,1,0:T(8,128)(2,1)S(1)} %get-tuple-element.30.land, f32[2,8,128]{2,1,0:T(8,128)S(1)} %get-tuple-element.31.rate), custom_call_target="tpu_custom_call" | custom-call | tf_op jit(solution)/shard_map/write/pallas_call | solution.py:531
  84.3 0.0 collective-permute-done.given
  84.3 3.6 %place.1 = bf16[192,65536]{1,0:T(8,128)(2,1)} custom-call(bf16[17,8,32768]{2,1,0:T(8,128)(2,1)S(1)} %collective-permute-done.given, bf16[192,65536]{1,0:T(8,128)(2,1)} %get-tuple-element.32.params_in), custom_call_target="tpu_custom_call", output_to_operand_aliasing={{}: (1, {})} | custom-call | tf_op jit(solution)/shard_map/place/pallas_call | solution.py:541
Async XLA Ops:
  70.2 14.1 %collective-permute-start = (bf16[17,8,32768]{2,1,0:T(8,128)(2,1)}, bf16[17,8,32768]{2,1,0:T(8,128)(2,1)S(1)}, u32[]{:S(2)}, u32[]{:S(2)}) collective-permute-start(bf16[17,8,32768]{2,1,0:T(8,128)(2,1)} %get-tuple-element.29), channel_id=1, source_target_pairs={{0,1},{1,0},{2,3},{3,2},{4,5},{5,4},{6,7},{7,6}} | collective-permute-start | bytes 26738696 | tf_op jit(solution)/shard_map/ppermute | solution.py:529
